TPU v7x, 512 devices: a whole 4x8x8 slice. The times are simulated.
512 devices in a mesh: expert: 8 (over x, core), dp: 64 (over z, y).
Axes of the slice: x: 4, y: 8, z: 8, core: 2. Of those that a mesh axis runs over, the one named last changes fastest.
Arguments:
- tokens: bfloat16 [4096, 4096], P(('expert', 'dp')), may hold values from -6 to 6
- expert_ids: int32 [4096, 2], P(('expert', 'dp')), may hold values from 0 to 7, as said below
- slots: int32 [4096, 2], P(('expert', 'dp')), may hold values from -1 to 1, as said below
- mix_weights: float32 [4096, 2], P(('expert', 'dp')), may hold values from 0.1 to 1
- w_gate: bfloat16 [8, 4096, 8192], P('expert', None, 'dp'), may hold values from -0.09375 to 0.09375
- w_up: bfloat16 [8, 4096, 8192], P('expert', None, 'dp'), may hold values from -0.09375 to 0.09375
- w_down: bfloat16 [8, 8192, 4096], P('expert', None, 'dp'), may hold values from -0.0625 to 0.0625
Outputs:
- mixed: bfloat16 [4096, 4096], P(('expert', 'dp'))
Inputs may be any that keep to these rules, and one draw needn't show every extreme that they name: `expert_ids`: each token names 2 different experts. Within each aligned block of 8 tokens (the tokens of one device), the assignments to one expert get distinct slots among 0 to 1 in some order, at most 2 of them are kept and the others get -1; an expert with 2 or more assignments in the block has all 2 slots used. No two assignments of one block share an expert and a slot. In every block some expert has all 2 slots used.
All inputs are finite; a program needn't handle non-finite values.
Results may differ from a plain program's by a relative error of at most 0.0085.
Values may be sent and summed in bfloat16 or wider, within the bound.
No kernel may reach another device: no remote copies, remote signals or barrier semaphores. Data moves between devices by JAX's collectives and lax.ppermute only.
A program may use at most 128 MiB of HBM per device.

v0:
```python
import jax
import jax.numpy as jnp
from jax import lax
from jax.sharding import PartitionSpec as P

CAP = 2


def shards(tokens, expert_ids, slots, mix_weights, w_gate, w_up, w_down):
    tok_rows, model_width = tokens.shape
    experts = lax.axis_size("expert")
    capacity = CAP
    slot_count = experts * capacity
    slot_ids = jnp.arange(slot_count, dtype=jnp.int32)
    slot_expert = slot_ids // capacity
    slot_index = slot_ids % capacity
    matches = (expert_ids[None, :, :] == slot_expert[:, None, None]) & (
        slots[None, :, :] == slot_index[:, None, None]
    )
    occupied = jnp.any(matches, axis=2)
    dispatch_table = occupied.astype(jnp.bfloat16)
    outgoing = jnp.dot(dispatch_table, tokens, preferred_element_type=jnp.float32).astype(
        jnp.bfloat16
    )
    arrived = lax.all_to_all(outgoing, "expert", split_axis=0, concat_axis=0, tiled=True)
    gate_w = w_gate[0]
    up_w = w_up[0]
    down_w = w_down[0]
    portion = lax.all_gather(arrived, "dp", axis=0, tiled=True)
    gate_part = jnp.dot(portion, gate_w, preferred_element_type=jnp.float32)
    up_part = jnp.dot(portion, up_w, preferred_element_type=jnp.float32)
    hidden = (jax.nn.silu(gate_part) * up_part).astype(jnp.bfloat16)
    summed = jnp.dot(
        lax.all_gather(hidden, "dp", axis=1, tiled=True), down_w, preferred_element_type=jnp.float32
    )
    result = summed.astype(jnp.bfloat16)
    groups = lax.axis_size("dp")
    blocks = result.reshape(groups, experts, capacity, result.shape[1])
    blocks = lax.all_to_all(blocks, "expert", split_axis=1, concat_axis=1, tiled=True)
    blocks = lax.all_to_all(blocks, "dp", split_axis=0, concat_axis=3, tiled=True)
    returned = blocks.reshape(slot_count, model_width)
    weight_table = jnp.sum(jnp.where(matches, mix_weights[None, :, :], 0.0), axis=2)
    mixed = jnp.dot(
        weight_table.T, returned.astype(jnp.float32), preferred_element_type=jnp.float32
    )
    return mixed.astype(jnp.bfloat16)


def solution(mesh):
    placed = (
        P(("expert", "dp"), None),
        P(("expert", "dp"), None),
        P(("expert", "dp"), None),
        P(("expert", "dp"), None),
        P("expert", None, "dp"),
        P("expert", None, "dp"),
        P("expert", None, "dp"),
    )
    return jax.shard_map(
        shards, mesh=mesh, in_specs=placed, out_specs=P(("expert", "dp"), None), check_vma=False
    )
```

profile of v0, /device:TPU:1, one launch (start us, length us, event | category | flops | bytes accessed | tf_op | source)
XLA Modules:
  0.0 327.1 jit_solution(15211576409830812576)
XLA Ops:
  6.5 0.0 copy-start
  6.5 0.0 copy-start.6
  6.5 0.0 all-gather.3.cloned.1.call-start
  6.5 0.9 fusion.5
  7.5 1.1 convolution_convert_fusion
  8.5 0.1 all_to_all.22
  8.6 14.5 %all_to_all.32 = bf16[8,2,4096]{2,1,0:T(2,128)(2,1)S(1)} all-to-all(bf16[8,2,4096]{2,1,0:T(2,128)(2,1)S(1)} %all_to_all.22), channel_id=1, replica_groups=mesh['expert'=8,'dp'=64] {'expert'}, dimensions={0} | all-to-all | bytes 262144 | tf_op jit(solution)/shard_map/all_to_all | solution.py:25
  23.1 0.7 all_to_all.24
  23.8 0.0 all-gather.3.cloned.1.call-update
  23.8 0.0 all-gather.5.cloned.1.call-start
  23.9 98.3 %all-gather.3.cloned.1.call-done = bf16[1024,4096]{1,0:T(8,128)(2,1)} async-done(((bf16[16,4096]{1,0:T(8,128)(2,1)}), bf16[1024,4096]{1,0:T(8,128)(2,1)}) %all-gather.3.cloned.1.call-update) | async-done | bytes 8388624 | tf_op jit(solution)/shard_map/all_gather | solution.py:29
  122.2 0.0 copy-done
  122.2 0.0 copy-start.5
  122.2 5.8 %fusion.3 = f32[1024,128]{1,0:T(8,128)S(1)} fusion(bf16[1024,4096]{1,0:T(8,128)(2,1)} %all-gather.3.cloned.1.call-done, bf16[1,4096,128]{2,1,0:T(8,128)(2,1)S(1)} %copy-done), kind=kOutput, calls=%fused_computation.7 | convolution fusion | flops 1073741824 | bytes 9961472 | tf_op jit(solution)/shard_map/dot_general | solution.py:30
  128.1 0.0 copy-done.6
  128.1 0.0 copy-done.5
  128.1 0.0 copy-start.1
  128.1 3.0 fusion
  131.1 0.0 all-gather.5.cloned.1.call-update
  131.2 0.0 copy-start.2
  131.2 0.0 copy-start.3
  131.2 0.0 copy-start.4
  131.2 141.9 %all-gather.5.cloned.1.call-done = bf16[1024,8192]{1,0:T(8,128)(2,1)} async-done(((bf16[1024,128]{1,0:T(8,128)(2,1)}), bf16[1024,8192]{1,0:T(8,128)(2,1)}) %all-gather.5.cloned.1.call-update) | async-done | bytes 16777232 | tf_op jit(solution)/shard_map/all_gather | solution.py:34
  273.1 0.0 copy-done.1
  273.1 10.9 %convolution_convert_fusion.2 = bf16[1024,64]{0,1:T(8,128)(2,1)S(1)} fusion(bf16[1024,8192]{1,0:T(8,128)(2,1)} %all-gather.5.cloned.1.call-done, bf16[1,8192,64]{1,2,0:T(8,128)(2,1)S(1)} %copy-done.1), kind=kOutput, calls=%fused_computation.4 | convolution fusion | flops 1073807360 | bytes 17956864 | tf_op jit(solution)/shard_map/dot_general | solution.py:33
  284.1 0.2 copy.29
  284.3 0.2 copy.34
  284.4 0.2 reshape.36
  284.7 13.9 %all_to_all.33 = bf16[8,2,4096]{2,1,0:T(2,128)(2,1)S(1)} all-to-all(bf16[8,2,4096]{2,1,0:T(2,128)(2,1)S(1)} %reshape.36), channel_id=1, replica_groups=mesh['expert'=8,'dp'=64] {'expert'}, dimensions={0} | all-to-all | bytes 262144 | tf_op jit(solution)/shard_map/all_to_all | solution.py:39
  298.6 0.2 reshape.37
  298.9 0.2 copy.31
  299.0 0.8 reshape.38
  299.9 7.4 %all-to-all-start.2 = ((bf16[64,2,512]{2,1,0:T(2,128)(2,1)}), bf16[64,2,512]{2,1,0:T(2,128)(2,1)S(1)}, u32[]{:S(2)}, u32[]{:S(2)}) async-start(bf16[64,2,512]{2,1,0:T(2,128)(2,1)} %reshape.38), calls=%async_computation.2 | async-start | bytes 262144 | tf_op jit(solution)/shard_map/all_to_all | solution.py:40
  307.2 0.0 copy-done.2
  307.3 0.0 copy-done.3
  307.3 0.0 copy-done.4
  307.3 0.1 select_reduce_fusion
  307.4 11.5 %all-to-all-done.2 = bf16[64,2,512]{2,1,0:T(2,128)(2,1)S(1)} async-done(((bf16[64,2,512]{2,1,0:T(2,128)(2,1)}), bf16[64,2,512]{2,1,0:T(2,128)(2,1)S(1)}, u32[]{:S(2)}, u32[]{:S(2)}) %all-to-all-start.2) | async-done | bytes 131104 | tf_op jit(solution)/shard_map/all_to_all | solution.py:40
  318.9 0.2 reshape.39
  319.1 0.1 copy.32
  319.2 0.3 reshape.35
  319.4 0.8 fusion.6
  (1 shorter events, 0.0 us)
Async XLA Ops:
  6.5 115.7 %copy-start = (bf16[1,4096,128]{2,1,0:T(8,128)(2,1)S(1)}, bf16[1,4096,128]{2,1,0:T(8,128)(2,1)}, u32[]{:S(2)}) copy-start(bf16[1,4096,128]{2,1,0:T(8,128)(2,1)} %param.11) | copy-start | bytes 3145732
  6.5 121.5 %copy-start.6 = (bf16[1,4096,128]{2,1,0:T(8,128)(2,1)S(1)}, bf16[1,4096,128]{2,1,0:T(8,128)(2,1)}, u32[]{:S(2)}) copy-start(bf16[1,4096,128]{2,1,0:T(8,128)(2,1)} %param.12) | copy-start | bytes 3145732
  6.5 115.7 %all-gather.3.cloned.1.call-start = ((), (), s32[]{:S(2)}) async-start(), calls=%async_computation.3 | async-start | bytes 8519680 | tf_op jit(solution)/shard_map/all_gather | solution.py:29
  23.8 249.3 %all-gather.5.cloned.1.call-start = ((), (), s32[]{:S(2)}) async-start(), calls=%async_computation.4 | async-start | bytes 17039360 | tf_op jit(solution)/shard_map/all_gather | solution.py:34
  122.2 5.9 %copy-start.5 = (bf16[1024,4096]{1,0:T(8,128)(2,1)S(1)}, bf16[1024,4096]{1,0:T(8,128)(2,1)}, u32[]{:S(2)}) copy-start(bf16[1024,4096]{1,0:T(8,128)(2,1)} %all-gather.3.cloned.1.call-done) | copy-start | bytes 25165828
  128.1 145.1 %copy-start.1 = (bf16[1,8192,64]{1,2,0:T(8,128)(2,1)S(1)}, bf16[1,8192,64]{1,2,0:T(8,128)(2,1)}, u32[]{:S(2)}) copy-start(bf16[1,8192,64]{1,2,0:T(8,128)(2,1)} %param.13) | copy-start | bytes 3145732
  131.2 176.1 %copy-start.2 = (s32[8,2]{0,1:T(2,128)S(1)}, s32[8,2]{0,1:T(2,128)}, u32[]{:S(2)}) copy-start(s32[8,2]{0,1:T(2,128)} %param.9) | copy-start | bytes 196
  131.2 176.1 %copy-start.3 = (s32[8,2]{0,1:T(2,128)S(1)}, s32[8,2]{0,1:T(2,128)}, u32[]{:S(2)}) copy-start(s32[8,2]{0,1:T(2,128)} %param.8) | copy-start | bytes 196
  131.2 176.1 %copy-start.4 = (f32[8,2]{0,1:T(2,128)S(1)}, f32[8,2]{0,1:T(2,128)}, u32[]{:S(2)}) copy-start(f32[8,2]{0,1:T(2,128)} %param.10) | copy-start | bytes 196
  299.9 19.0 %all-to-all-start.2 = ((bf16[64,2,512]{2,1,0:T(2,128)(2,1)}), bf16[64,2,512]{2,1,0:T(2,128)(2,1)S(1)}, u32[]{:S(2)}, u32[]{:S(2)}) async-start(bf16[64,2,512]{2,1,0:T(2,128)(2,1)} %reshape.38), calls=%async_computation.2 | async-start | bytes 262144 | tf_op jit(solution)/shard_map/all_to_all | solution.py:40
Sparse Core Ops, SparseCore 0:
  24.0 98.1 all-gather.2
  131.3 141.7 all-gather.4
where the time goes:
time: 327 us
  waiting for transfers between devices  252 us (77%)
  blocking collectives  28.4 us (9%)
  matrix products  21.7 us (7%)
  between operations  13.6 us (4%)
  starting transfers between devices  7.4 us (2%)
    all_gather x1, waiting for transfers between devices, shards(): lax.all_gather(hidden, 'dp', axis=1, tiled=True)  142 us
    all_gather x1, waiting for transfers between devices, shards(): portion = lax.all_gather(arrived, 'dp', axis=0, tiled=True)  98.3 us
    all_to_all x1, blocking collectives, shards(): lax.all_to_all(outgoing, 'expert', split_axis=0, concat_axis=0, tiled=True)  14.5 us
    all_to_all x1, blocking collectives, shards(): lax.all_to_all(blocks, 'expert', split_axis=1, concat_axis=1, tiled=True)  13.9 us
    all_to_all x1, waiting for transfers between devices, shards(): lax.all_to_all(blocks, 'dp', split_axis=0, concat_axis=3, tiled=True)  11.5 us
    dot_general x1, matrix products, shards(): jnp.dot(lax.all_gather(hidden, 'dp', axis=1, tiled=True), down_w, preferr...  10.9 us
    all_to_all x1, starting transfers between devices, shards(): lax.all_to_all(blocks, 'dp', split_axis=0, concat_axis=3, tiled=True)  7.36 us
  transfers between devices with their start and end apart: 3, of which 3 were waited for; matrix products, arithmetic and copies ran while one was open for 0% of the time, Pallas kernels for 0%

commit v1 on v0

v1 whole, which is shorter than its diff:
```python
import jax
import jax.numpy as jnp
from jax import lax
from jax.sharding import Mesh, PartitionSpec as P

CAP = 2
LANES = 128
STEPS = (64, 32, 16, 8)
GROUP = ("x", "core")
PLANE = ("z", "y")


def raise_rows(peak):
    k = jnp.zeros_like(peak)
    for p in STEPS:
        low = peak < 2.0 ** (15 - p)
        peak = jnp.where(low, peak * 2.0**p, peak)
        k = jnp.where(low, k + p, k)
    return k


def power(k, sign):
    out = jnp.ones_like(k)
    for p in STEPS:
        low = k >= p
        out = jnp.where(low, out * 2.0 ** (sign * p), out)
        k = jnp.where(low, k - p, k)
    return out


def shards(tokens, expert_ids, slots, mix_weights, w_gate, w_up, w_down):
    tok_rows, width = tokens.shape
    experts = lax.axis_size(GROUP)
    nz, ny = lax.axis_size("z"), lax.axis_size("y")
    slot_count = experts * CAP
    rows = nz * ny * slot_count
    unit = w_gate.shape[2]
    cols = w_down.shape[2]

    wd = w_down[0].T.reshape(cols, nz, ny, unit).transpose(2, 0, 1, 3)
    wd = lax.all_to_all(wd, "y", split_axis=0, concat_axis=0, tiled=True)
    wd = wd.reshape(ny * cols, nz * unit)

    slot_ids = jnp.arange(slot_count, dtype=jnp.int32)
    matches = (expert_ids[None, :, :] == (slot_ids // CAP)[:, None, None]) & (
        slots[None, :, :] == (slot_ids % CAP)[:, None, None]
    )
    table = jnp.any(matches, axis=2).astype(jnp.bfloat16)
    wide = tokens.astype(jnp.float32)
    k = raise_rows(jnp.max(jnp.abs(wide), axis=1, keepdims=True))
    lifted = (wide * power(k, 1)).astype(jnp.bfloat16)
    held = jnp.concatenate(
        [lifted, jnp.broadcast_to(k, (tok_rows, LANES)).astype(jnp.bfloat16)], axis=1
    )
    outgoing = jnp.dot(table, held, preferred_element_type=jnp.float32).astype(jnp.float16)
    arrived = lax.all_to_all(outgoing, GROUP, split_axis=0, concat_axis=0, tiled=True)
    portion = lax.all_gather(arrived, PLANE, axis=0, tiled=True)
    x = portion[:, :width].astype(jnp.bfloat16)
    lower = power(portion[:, width : width + 1].astype(jnp.float32), -1)

    gate = jnp.dot(x, w_gate[0], preferred_element_type=jnp.float32) * lower
    up = jnp.dot(x, w_up[0], preferred_element_type=jnp.float32) * lower
    hidden = jax.nn.silu(gate) * up
    hidden = hidden * 2.0**-8
    hk = raise_rows(jnp.max(jnp.abs(hidden), axis=1))
    packed = (hidden * power(hk, 1)[:, None]).astype(jnp.float16)
    packed = jnp.concatenate([packed, hk.reshape(rows // LANES, LANES).astype(jnp.float16)], axis=0)
    spread = lax.all_gather(packed, "z", axis=0, tiled=False)
    drop = power(spread[:, rows:].astype(jnp.float32).reshape(nz, rows), -1) * 2.0**8
    h = (spread[:, :rows].astype(jnp.float32) * drop[:, :, None]).astype(jnp.bfloat16)
    h = h.transpose(1, 0, 2).reshape(rows, nz * unit)
    part = lax.dot_general(
        h, wd, (((1,), (1,)), ((), ())), preferred_element_type=jnp.float32
    ).astype(jnp.bfloat16)
    part = part.reshape(nz * ny, slot_count, ny * cols)
    part = lax.all_to_all(part, PLANE, split_axis=0, concat_axis=0, tiled=True)
    part = part.reshape(nz, ny, slot_count, ny * cols).astype(jnp.float32).sum(axis=1)
    result = part.transpose(1, 0, 2).reshape(slot_count, width).astype(jnp.bfloat16)
    back = lax.all_to_all(result, GROUP, split_axis=0, concat_axis=0, tiled=True)
    weights = jnp.sum(jnp.where(matches, mix_weights[None, :, :], 0.0), axis=2)
    mixed = jnp.dot(weights.T, back.astype(jnp.float32), preferred_element_type=jnp.float32)
    return mixed.astype(jnp.bfloat16)


def solution(mesh):
    experts, dp = mesh.devices.shape
    ny = 8 if dp % 8 == 0 else 1
    split = Mesh(
        mesh.devices.reshape(experts // 2, 2, dp // ny, ny), ("x", "core", "z", "y")
    )
    tok = P(GROUP + PLANE, None)
    weight = P(GROUP, None, PLANE)
    return jax.shard_map(
        shards,
        mesh=split,
        in_specs=(tok, tok, tok, tok, weight, weight, weight),
        out_specs=tok,
        check_vma=False,
    )
```

time: 327 us -> 202 us (0.62)
  waiting for transfers between devices: 252 us -> 7.82 us
  blocking collectives: 28.4 us -> 137 us
  starting transfers between devices: 7.4 us -> 31.1 us
  matrix products: 21.7 us -> 8.29 us
  between operations: 13.6 us -> 0.19 us
  local copies, waits for them, and re-layouts: 3.24 us -> 10.4 us
  other arithmetic: 1 us -> 5.96 us
    all_gather x2 -> x0, waiting for transfers between devices: 240 us -> none  [the longest x1 142 us: shards(): lax.all_gather(hidden, 'dp', axis=1, tiled=True)]
    all_gather x0 -> x2, blocking collectives: none -> 113 us  [the longest x1 87.6 us: shards(): portion = lax.all_gather(arrived, PLANE, axis=0, tiled=True)]
    all_to_all x1 -> x3, starting transfers between devices: 7.36 us -> 31.1 us  [the longest x1 16.7 us: shards(): lax.all_to_all(result, GROUP, split_axis=0, concat_axis=0, tiled=True)]
    dot_general x5, matrix products: 21.7 us -> 8.29 us  [the longest x1 2.54 us: shards(): lax.dot_general(h, wd, (((1,), (1,)), ((), ())), preferred_element_type=j...]
    unnamed x18 -> x12, local copies, waits for them, and re-layouts: 1.53 us -> 5.76 us
    all_to_all x1 -> x3, waiting for transfers between devices: 11.5 us -> 7.82 us  [the longest x1 5.17 us: shards(): lax.all_to_all(result, GROUP, split_axis=0, concat_axis=0, tiled=True)]
    all_to_all x2 -> x1, blocking collectives: 28.4 us -> 24.9 us  [shards(): part = lax.all_to_all(part, PLANE, split_axis=0, concat_axis=0, tiled=True)]
    convert_element_type x0 -> x4, other arithmetic: none -> 3.34 us  [the longest x1 2.21 us: shards(): (spread[:, :rows].astype(jnp.float32) * drop[:, :, None]).astype(jnp.bflo...]
  transfers between devices with their start and end apart: 3 -> 3, of which waited for: 3 -> 2; matrix products, arithmetic and copies ran while one was open for 0% -> 8% of each run, Pallas kernels for 0% -> 0%
where the time goes in v1:
time: 202 us; the launch traced here: 201 us
  blocking collectives  137 us (68%)
  starting transfers between devices  31.1 us (15%)
  local copies, waits for them, and re-layouts  10.4 us (5%)
  matrix products  8.29 us (4%)
  waiting for transfers between devices  7.82 us (4%)
  other arithmetic  5.96 us (3%)
    all_gather x1, blocking collectives, shards(): portion = lax.all_gather(arrived, PLANE, axis=0, tiled=True)  87.6 us
    all_gather x1, blocking collectives, shards(): spread = lax.all_gather(packed, 'z', axis=0, tiled=False)  25 us
    all_to_all x1, blocking collectives, shards(): part = lax.all_to_all(part, PLANE, split_axis=0, concat_axis=0, tiled=True)  24.9 us
    all_to_all x1, starting transfers between devices, shards(): lax.all_to_all(result, GROUP, split_axis=0, concat_axis=0, tiled=True)  16.7 us
    all_to_all x1, starting transfers between devices, shards(): lax.all_to_all(outgoing, GROUP, split_axis=0, concat_axis=0, tiled=True)  10.1 us
    unnamed x12, local copies, waits for them, and re-layouts  5.76 us
    all_to_all x1, waiting for transfers between devices, shards(): lax.all_to_all(result, GROUP, split_axis=0, concat_axis=0, tiled=True)  5.17 us
    all_to_all x1, starting transfers between devices, shards(): wd = lax.all_to_all(wd, 'y', split_axis=0, concat_axis=0, tiled=True)  4.23 us
  transfers between devices with their start and end apart: 3, of which 2 were waited for; matrix products, arithmetic and copies ran while one was open for 8% of the time, Pallas kernels for 0%

profile of v1, /device:TPU:1, one launch (start us, length us, event | category | flops | bytes accessed | tf_op | source)
XLA Modules:
  0.0 201.1 jit_solution(5151954368297772800)
XLA Ops:
  0.0 0.0 copy-start
  0.0 1.0 fusion.11
  1.1 0.9 fusion.12
  2.0 0.8 fusion.18
  2.8 0.1 broadcast_in_dim.41
  2.8 0.2 convolution_convert_fusion
  3.1 0.7 all_to_all.20
  3.8 10.1 %all-to-all-start = ((f16[8,2,4224]{2,1,0:T(2,128)(2,1)}), f16[8,2,4224]{2,1,0:T(2,128)(2,1)S(1)}, u32[]{:S(2)}, u32[]{:S(2)}) async-start(f16[8,2,4224]{2,1,0:T(2,128)(2,1)} %all_to_all.20), calls=%async_computation | async-start | bytes 270336 | tf_op jit(solution)/shard_map/all_to_all | solution.py:56
  13.9 1.5 copy.33
  15.4 1.2 copy.41
  16.6 2.7 %all-to-all-done = f16[8,2,4224]{2,1,0:T(2,128)(2,1)S(1)} async-done(((f16[8,2,4224]{2,1,0:T(2,128)(2,1)}), f16[8,2,4224]{2,1,0:T(2,128)(2,1)S(1)}, u32[]{:S(2)}, u32[]{:S(2)}) %all-to-all-start) | async-done | bytes 135200 | tf_op jit(solution)/shard_map/all_to_all | solution.py:56
  19.2 4.2 %all-to-all-start.1 = ((bf16[8,64,8,128]{3,2,1,0:T(8,128)(2,1)}), bf16[8,64,8,128]{3,2,1,0:T(8,128)(2,1)}, u32[]{:S(2)}, u32[]{:S(2)}) async-start(bf16[8,64,8,128]{3,2,1,0:T(8,128)(2,1)} %bitcast.61), calls=%async_computation.1 | async-start | bytes 2097152 | tf_op jit(solution)/shard_map/all_to_all | solution.py:41
  23.4 0.1 all_to_all.22
  23.5 0.0 copy-start.4
  23.5 87.6 %all-gather.3 = f16[1024,4224]{1,0:T(8,128)(2,1)S(1)} all-gather(f16[16,4224]{1,0:T(8,128)(2,1)S(1)} %all_to_all.22), channel_id=1, replica_groups=mesh['x'=4,'core'=2,'z'=8,'y'=8] {'z','y'}, dimensions={0}, use_global_device_ids=true | all-gather | bytes 8785920 | tf_op jit(solution)/shard_map/all_gather | solution.py:57
  111.1 0.4 fusion.10
  111.5 0.0 copy-done.4
  111.5 2.3 %fusion.2 = f32[1024,128]{1,0:T(8,128)S(1)} fusion(f16[1024,4224]{1,0:T(8,128)(2,1)S(1)} %all-gather.3, bf16[1,4096,128]{2,1,0:T(8,128)(2,1)S(1)} %copy-done.4, f32[1024]{0:T(1024)S(1)} %fusion.10), kind=kOutput, calls=%fused_computation.7 | convolution fusion | flops 1078067200 | bytes 9965568 | tf_op jit(solution)/shard_map/dot_general | solution.py:61
  113.8 0.0 copy-done
  113.9 2.4 %abs_reduce_fusion = (f32[1024]{0:T(1024)S(1)}, f32[1024,128]{1,0:T(8,128)S(1)}) fusion(f32[1024]{0:T(1024)S(1)} %fusion.10, bf16[1,4096,128]{2,1,0:T(8,128)(2,1)S(1)} %copy-done, f16[1024,4224]{1,0:T(8,128)(2,1)S(1)} %all-gather.3, f32[1024,128]{1,0:T(8,128)S(1)} %fusion.2), kind=kOutput, calls=%fused_computation.25 | convolution fusion | flops 1079114752 | bytes 10493952 | tf_op jit(solution)/shard_map/dot_general | solution.py:62
  116.3 0.2 multiply_convert_fusion.1
  116.5 0.1 pad_maximum_fusion
  116.6 25.0 %all-gather.4 = f16[8256,128]{1,0:T(8,128)(2,1)S(1)} all-gather(f16[1032,128]{1,0:T(8,128)(2,1)S(1)} %pad_maximum_fusion), channel_id=2, replica_groups=mesh['x'=4,'core'=2,'z'=8,'y'=8] {'z'}, dimensions={0}, use_global_device_ids=true | all-gather | bytes 2377728 | tf_op jit(solution)/shard_map/all_gather | solution.py:68
  141.6 1.8 slice.18
  143.4 4.2 %copy.31 = f16[8,1024,128]{1,2,0:T(8,128)(2,1)} copy(f16[8,1024,128]{2,1,0:T(8,128)(2,1)} %slice.18) | data formatting | bytes 4194304
  147.6 2.2 %multiply_convert_fusion = bf16[8,1024,128]{1,2,0:T(8,128)(2,1)S(1)} fusion(f16[8,1024,128]{1,2,0:T(8,128)(2,1)} %copy.31, f32[8,1024]{1,0:T(8,128)S(1)} %fusion.17), kind=kLoop, calls=%fused_computation.5 | loop fusion | flops 3145728 | bytes 4227072 | tf_op jit(solution)/shard_map/convert_element_type | solution.py:70
  149.9 0.0 all-to-all-done.1
  149.9 0.0 copy-start.1
  149.9 0.0 copy-start.2
  149.9 0.0 copy-start.3
  149.9 2.5 %convolution_convert_fusion.2 = bf16[1024,512]{1,0:T(8,128)(2,1)S(1)} fusion(bf16[1024,1024]{0,1:T(8,128)(2,1)S(1)} %bitcast.65, bf16[64,8,8,128]{3,2,1,0:T(8,128)(2,1)} %bitcast.20), kind=kOutput, calls=%fused_computation.6 | convolution fusion | flops 1074266112 | bytes 4194304 | tf_op jit(solution)/shard_map/dot_general | solution.py:72
  152.5 24.9 %all_to_all.31 = bf16[64,16,512]{2,1,0:T(8,128)(2,1)S(1)} all-to-all(bf16[64,16,512]{2,1,0:T(8,128)(2,1)S(1)} %bitcast.67), channel_id=1, replica_groups=mesh['x'=4,'core'=2,'z'=8,'y'=8] {'z','y'}, dimensions={0} | all-to-all | bytes 2097152 | tf_op jit(solution)/shard_map/all_to_all | solution.py:76
  177.4 0.2 bitcast_reduce_fusion
  177.5 0.1 copy.30
  177.6 0.7 convert_element_type.71
  178.3 16.7 %all-to-all-start.3 = ((bf16[8,2,4096]{2,1,0:T(2,128)(2,1)}), bf16[8,2,4096]{2,1,0:T(2,128)(2,1)S(1)}, u32[]{:S(2)}, u32[]{:S(2)}) async-start(bf16[8,2,4096]{2,1,0:T(2,128)(2,1)} %convert_element_type.71), calls=%async_computation.3 | async-start | bytes 262144 | tf_op jit(solution)/shard_map/all_to_all | solution.py:79
  195.0 0.0 copy-done.1
  195.0 0.0 copy-done.2
  195.0 0.0 copy-done.3
  195.1 0.1 select_reduce_fusion
  195.1 5.2 %all-to-all-done.3 = bf16[8,2,4096]{2,1,0:T(2,128)(2,1)S(1)} async-done(((bf16[8,2,4096]{2,1,0:T(2,128)(2,1)}), bf16[8,2,4096]{2,1,0:T(2,128)(2,1)S(1)}, u32[]{:S(2)}, u32[]{:S(2)}) %all-to-all-start.3) | async-done | bytes 131104 | tf_op jit(solution)/shard_map/all_to_all | solution.py:79
  200.3 0.1 all_to_all.26
  200.4 0.8 fusion.25
  (6 shorter events, 0.1 us)
Async XLA Ops:
  0.0 113.8 %copy-start = (bf16[1,4096,128]{2,1,0:T(8,128)(2,1)S(1)}, bf16[1,4096,128]{2,1,0:T(8,128)(2,1)}, u32[]{:S(2)}) copy-start(bf16[1,4096,128]{2,1,0:T(8,128)(2,1)} %param.12) | copy-start | bytes 3145732
  3.8 15.4 %all-to-all-start = ((f16[8,2,4224]{2,1,0:T(2,128)(2,1)}), f16[8,2,4224]{2,1,0:T(2,128)(2,1)S(1)}, u32[]{:S(2)}, u32[]{:S(2)}) async-start(f16[8,2,4224]{2,1,0:T(2,128)(2,1)} %all_to_all.20), calls=%async_computation | async-start | bytes 270336 | tf_op jit(solution)/shard_map/all_to_all | solution.py:56
  19.2 130.7 %all-to-all-start.1 = ((bf16[8,64,8,128]{3,2,1,0:T(8,128)(2,1)}), bf16[8,64,8,128]{3,2,1,0:T(8,128)(2,1)}, u32[]{:S(2)}, u32[]{:S(2)}) async-start(bf16[8,64,8,128]{3,2,1,0:T(8,128)(2,1)} %bitcast.61), calls=%async_computation.1 | async-start | bytes 2097152 | tf_op jit(solution)/shard_map/all_to_all | solution.py:41
  23.5 88.0 %copy-start.4 = (bf16[1,4096,128]{2,1,0:T(8,128)(2,1)S(1)}, bf16[1,4096,128]{2,1,0:T(8,128)(2,1)}, u32[]{:S(2)}) copy-start(bf16[1,4096,128]{2,1,0:T(8,128)(2,1)} %param.11) | copy-start | bytes 3145732
  149.9 45.2 %copy-start.1 = (s32[8,2]{0,1:T(2,128)S(1)}, s32[8,2]{0,1:T(2,128)}, u32[]{:S(2)}) copy-start(s32[8,2]{0,1:T(2,128)} %param.9) | copy-start | bytes 196
  149.9 45.2 %copy-start.2 = (s32[8,2]{0,1:T(2,128)S(1)}, s32[8,2]{0,1:T(2,128)}, u32[]{:S(2)}) copy-start(s32[8,2]{0,1:T(2,128)} %param.8) | copy-start | bytes 196
  149.9 45.1 %copy-start.3 = (f32[8,2]{0,1:T(2,128)S(1)}, f32[8,2]{0,1:T(2,128)}, u32[]{:S(2)}) copy-start(f32[8,2]{0,1:T(2,128)} %param.10) | copy-start | bytes 196
  178.3 22.0 %all-to-all-start.3 = ((bf16[8,2,4096]{2,1,0:T(2,128)(2,1)}), bf16[8,2,4096]{2,1,0:T(2,128)(2,1)S(1)}, u32[]{:S(2)}, u32[]{:S(2)}) async-start(bf16[8,2,4096]{2,1,0:T(2,128)(2,1)} %convert_element_type.71), calls=%async_computation.3 | async-start | bytes 262144 | tf_op jit(solution)/shard_map/all_to_all | solution.py:79

commit v2 on v1

--- a/solution.py
+++ b/solution.py
@@ -1,9 +1,12 @@
 import jax
 import jax.numpy as jnp
 from jax import lax
+from jax.experimental import pallas as pl
+from jax.experimental.pallas import tpu as pltpu
 from jax.sharding import Mesh, PartitionSpec as P
 
 CAP = 2
+BLOCK = 256
 LANES = 128
 STEPS = (64, 32, 16, 8)
 GROUP = ("x", "core")
@@ -28,18 +31,47 @@
     return out
 
 
+def down_kernel(h_ref, w_ref, o_ref, w_all):
+    nz, rows, unit = h_ref.shape
+    ny, _, cols, _ = w_ref.shape
+    for z in range(nz):
+        for y in range(ny):
+            w_all[pl.ds(y * cols, cols), pl.ds(z * unit, unit)] = w_ref[y, z]
+
+    @pl.loop(0, rows // BLOCK)
+    def _(i):
+        at = pl.ds(pl.multiple_of(i * BLOCK, BLOCK), BLOCK)
+        h = jnp.concatenate([h_ref[z, at, :] for z in range(nz)], axis=1)
+        o_ref[at, :] = lax.dot_general(
+            h, w_all[...], (((1,), (1,)), ((), ())), preferred_element_type=jnp.float32
+        ).astype(o_ref.dtype)
+
+
+def down(h, w):
+    nz, rows, unit = h.shape
+    ny, _, cols, _ = w.shape
+    return pl.pallas_call(
+        down_kernel,
+        out_shape=jax.ShapeDtypeStruct((rows, ny * cols), jnp.bfloat16),
+        in_specs=[pl.BlockSpec(memory_space=pltpu.VMEM)] * 2,
+        out_specs=pl.BlockSpec(memory_space=pltpu.VMEM),
+        compiler_params=pltpu.CompilerParams(vmem_limit_bytes=16 << 20),
+        scratch_shapes=[pltpu.VMEM((ny * cols, nz * unit), jnp.bfloat16)],
+        cost_estimate=pl.CostEstimate(
+            flops=2 * rows * nz * unit * ny * cols, bytes_accessed=4 << 20, transcendentals=0
+        ),
+    )(h, w)
+
+
 def shards(tokens, expert_ids, slots, mix_weights, w_gate, w_up, w_down):
     tok_rows, width = tokens.shape
     experts = lax.axis_size(GROUP)
     nz, ny = lax.axis_size("z"), lax.axis_size("y")
     slot_count = experts * CAP
-    rows = nz * ny * slot_count
     unit = w_gate.shape[2]
     cols = w_down.shape[2]
 
-    wd = w_down[0].T.reshape(cols, nz, ny, unit).transpose(2, 0, 1, 3)
-    wd = lax.all_to_all(wd, "y", split_axis=0, concat_axis=0, tiled=True)
-    wd = wd.reshape(ny * cols, nz * unit)
+    wd = w_down[0].T.reshape(cols, nz, ny, unit).transpose(2, 1, 0, 3)
 
     slot_ids = jnp.arange(slot_count, dtype=jnp.int32)
     matches = (expert_ids[None, :, :] == (slot_ids // CAP)[:, None, None]) & (
@@ -61,17 +93,14 @@
     gate = jnp.dot(x, w_gate[0], preferred_element_type=jnp.float32) * lower
     up = jnp.dot(x, w_up[0], preferred_element_type=jnp.float32) * lower
     hidden = jax.nn.silu(gate) * up
-    hidden = hidden * 2.0**-8
-    hk = raise_rows(jnp.max(jnp.abs(hidden), axis=1))
-    packed = (hidden * power(hk, 1)[:, None]).astype(jnp.float16)
-    packed = jnp.concatenate([packed, hk.reshape(rows // LANES, LANES).astype(jnp.float16)], axis=0)
+    packed = jnp.sqrt(jnp.sqrt(jnp.abs(hidden * 2.0**40)))
+    packed = jnp.where(hidden < 0, -packed, packed).astype(jnp.float16)
+    packed, wd = lax.optimization_barrier((packed, wd))
+    wd = lax.all_to_all(wd, "y", split_axis=0, concat_axis=0, tiled=True)
     spread = lax.all_gather(packed, "z", axis=0, tiled=False)
-    drop = power(spread[:, rows:].astype(jnp.float32).reshape(nz, rows), -1) * 2.0**8
-    h = (spread[:, :rows].astype(jnp.float32) * drop[:, :, None]).astype(jnp.bfloat16)
-    h = h.transpose(1, 0, 2).reshape(rows, nz * unit)
-    part = lax.dot_general(
-        h, wd, (((1,), (1,)), ((), ())), preferred_element_type=jnp.float32
-    ).astype(jnp.bfloat16)
+    spread = spread.astype(jnp.float32)
+    h = (spread * jnp.abs(spread) * (spread * spread * 2.0**-40)).astype(jnp.bfloat16)
+    part = down(h, wd)
     part = part.reshape(nz * ny, slot_count, ny * cols)
     part = lax.all_to_all(part, PLANE, split_axis=0, concat_axis=0, tiled=True)
     part = part.reshape(nz, ny, slot_count, ny * cols).astype(jnp.float32).sum(axis=1)

time: 202 us -> 177 us (0.88)
  blocking collectives: 137 us -> 118 us
  local copies, waits for them, and re-layouts: 10.4 us -> 4.91 us
  Pallas kernels: 0 us -> 3.41 us
  matrix products: 8.29 us -> 5.95 us
    all_gather x1, blocking collectives: 87.6 us -> 64.3 us  [shards(): portion = lax.all_gather(arrived, PLANE, axis=0, tiled=True)]
    unnamed x12 -> x11, local copies, waits for them, and re-layouts: 5.76 us -> 1.52 us
    all_to_all x1, blocking collectives: 24.9 us -> 28.4 us  [shards(): part = lax.all_to_all(part, PLANE, split_axis=0, concat_axis=0, tiled=True)]
    pallas_call x0 -> x1, Pallas kernels: none -> 3.41 us  [down(): pl.pallas_call(down_kernel, out_shape=jax.ShapeDtypeStruct((rows, ny * co...]
    dot_general x1 -> x0, matrix products: 2.54 us -> none  [shards(): lax.dot_general(h, wd, (((1,), (1,)), ((), ())), preferred_element_type=j...]
  transfers between devices with their start and end apart: 3 -> 3, of which waited for: 2 -> 2; matrix products, arithmetic and copies ran while one was open for 8% -> 2% of each run, Pallas kernels for 0% -> 0%
where the time goes in v2:
time: 177 us; the launch traced here: 176 us
  blocking collectives  118 us (67%)
  starting transfers between devices  32.8 us (19%)
  waiting for transfers between devices  7.3 us (4%)
  matrix products  5.95 us (3%)
  local copies, waits for them, and re-layouts  4.91 us (3%)
  other arithmetic  4.36 us (2%)
  Pallas kernels  3.41 us (2%)
    all_gather x1, blocking collectives, shards(): portion = lax.all_gather(arrived, PLANE, axis=0, tiled=True)  64.3 us
    all_to_all x1, blocking collectives, shards(): part = lax.all_to_all(part, PLANE, split_axis=0, concat_axis=0, tiled=True)  28.4 us
    all_gather x1, blocking collectives, shards(): spread = lax.all_gather(packed, 'z', axis=0, tiled=False)  24.8 us
    all_to_all x1, starting transfers between devices, shards(): lax.all_to_all(result, GROUP, split_axis=0, concat_axis=0, tiled=True)  17.9 us
    all_to_all x1, starting transfers between devices, shards(): lax.all_to_all(outgoing, GROUP, split_axis=0, concat_axis=0, tiled=True)  10.1 us
    all_to_all x1, waiting for transfers between devices, shards(): lax.all_to_all(result, GROUP, split_axis=0, concat_axis=0, tiled=True)  5.17 us
    all_to_all x1, starting transfers between devices, shards(): wd = lax.all_to_all(wd, 'y', split_axis=0, concat_axis=0, tiled=True)  4.76 us
  transfers between devices with their start and end apart: 3, of which 2 were waited for; matrix products, arithmetic and copies ran while one was open for 2% of the time, Pallas kernels for 0%

profile of v2, /device:TPU:1, one launch (start us, length us, event | category | flops | bytes accessed | tf_op | source)
XLA Modules:
  0.0 176.4 jit_solution(10469013452107099239)
XLA Ops:
  0.0 0.0 copy-start
  0.0 1.0 fusion.15
  1.1 0.9 fusion.16
  2.0 0.8 fusion.20
  2.8 0.1 broadcast_in_dim.28
  2.8 0.2 convolution_convert_fusion
  3.1 0.7 all_to_all.20
  3.8 10.1 %all-to-all-start = ((f16[8,2,4224]{2,1,0:T(2,128)(2,1)}), f16[8,2,4224]{2,1,0:T(2,128)(2,1)S(1)}, u32[]{:S(2)}, u32[]{:S(2)}) async-start(f16[8,2,4224]{2,1,0:T(2,128)(2,1)} %all_to_all.20), calls=%async_computation | async-start | bytes 270336 | tf_op jit(solution)/shard_map/all_to_all | solution.py:88
  13.9 1.5 copy.27
  15.4 1.7 copy.29
  17.1 2.1 %all-to-all-done = f16[8,2,4224]{2,1,0:T(2,128)(2,1)S(1)} async-done(((f16[8,2,4224]{2,1,0:T(2,128)(2,1)}), f16[8,2,4224]{2,1,0:T(2,128)(2,1)S(1)}, u32[]{:S(2)}, u32[]{:S(2)}) %all-to-all-start) | async-done | bytes 135200 | tf_op jit(solution)/shard_map/all_to_all | solution.py:88
  19.2 0.1 all_to_all.22
  19.3 64.3 %all-gather.3 = f16[1024,4224]{1,0:T(8,128)(2,1)S(1)} all-gather(f16[16,4224]{1,0:T(8,128)(2,1)S(1)} %all_to_all.22), channel_id=1, replica_groups=mesh['x'=4,'core'=2,'z'=8,'y'=8] {'z','y'}, dimensions={0}, use_global_device_ids=true | all-gather | bytes 8785920 | tf_op jit(solution)/shard_map/all_gather | solution.py:89
  83.6 0.0 copy-start.4
  83.6 0.4 fusion.12
  84.0 0.0 copy-done
  84.0 2.3 %fusion.5 = f32[1024,128]{1,0:T(8,128)S(1)} fusion(f16[1024,4224]{1,0:T(8,128)(2,1)S(1)} %all-gather.3, bf16[1,4096,128]{2,1,0:T(8,128)(2,1)S(1)} %copy-done, f32[1024]{0:T(1024)S(1)} %fusion.12), kind=kOutput, calls=%fused_computation.11 | convolution fusion | flops 1078067200 | bytes 9965568 | tf_op jit(solution)/shard_map/dot_general | solution.py:93
  86.4 0.0 copy-done.4
  86.4 2.6 %fusion.11 = f16[1024,128]{1,0:T(8,128)(2,1)S(1)} fusion(bf16[1,4096,128]{2,1,0:T(8,128)(2,1)S(1)} %copy-done.4, f16[1024,4224]{1,0:T(8,128)(2,1)S(1)} %all-gather.3, f32[1024,128]{1,0:T(8,128)S(1)} %fusion.5, f32[1024]{0:T(1024)S(1)} %fusion.12), kind=kOutput, calls=%fused_computation.27 | convolution fusion | flops 1079508992 | bytes 10227712 | tf_op jit(solution)/shard_map/dot_general | solution.py:94
  89.0 0.0 copy-start.1
  89.0 0.0 copy-start.2
  89.0 0.0 copy-start.3
  89.0 4.8 %all-to-all-start.1 = ((bf16[8,8,64,128]{3,2,1,0:T(8,128)(2,1)}), bf16[8,8,64,128]{3,2,1,0:T(8,128)(2,1)}, u32[]{:S(2)}, u32[]{:S(2)}) async-start(bf16[8,8,64,128]{3,2,1,0:T(8,128)(2,1)} %bitcast.25), calls=%async_computation.1 | async-start | bytes 2097152 | tf_op jit(solution)/shard_map/all_to_all | solution.py:99
  93.8 24.8 %all-gather.4 = f16[8192,128]{1,0:T(8,128)(2,1)S(1)} all-gather(f16[1024,128]{1,0:T(8,128)(2,1)S(1)} %fusion.11), channel_id=2, replica_groups=mesh['x'=4,'core'=2,'z'=8,'y'=8] {'z'}, dimensions={0}, use_global_device_ids=true | all-gather | bytes 2359296 | tf_op jit(solution)/shard_map/all_gather | solution.py:100
  118.6 0.9 fusion.3.h_ref
  119.6 0.0 all-to-all-done.1.w_ref
  119.6 3.4 %shard_map.73 = bf16[1024,512]{1,0:T(8,128)(2,1)S(1)} custom-call(bf16[8,1024,128]{2,1,0:T(8,128)(2,1)S(1)} %fusion.3.h_ref, bf16[8,8,64,128]{3,2,1,0:T(8,128)(2,1)} %all-to-all-done.1.w_ref), custom_call_target="tpu_custom_call" | custom-call | flops 1073741824 | bytes 4194304 | tf_op jit(solution)/shard_map/pallas_call | solution.py:53
  123.0 28.4 %all_to_all.31 = bf16[64,16,512]{2,1,0:T(8,128)(2,1)S(1)} all-to-all(bf16[64,16,512]{2,1,0:T(8,128)(2,1)S(1)} %bitcast.26), channel_id=1, replica_groups=mesh['x'=4,'core'=2,'z'=8,'y'=8] {'z','y'}, dimensions={0} | all-to-all | bytes 2097152 | tf_op jit(solution)/shard_map/all_to_all | solution.py:105
  151.5 0.2 bitcast_reduce_fusion
  151.6 0.1 copy.26
  151.7 0.7 convert_element_type.62
  152.4 17.9 %all-to-all-start.3 = ((bf16[8,2,4096]{2,1,0:T(2,128)(2,1)}), bf16[8,2,4096]{2,1,0:T(2,128)(2,1)S(1)}, u32[]{:S(2)}, u32[]{:S(2)}) async-start(bf16[8,2,4096]{2,1,0:T(2,128)(2,1)} %convert_element_type.62), calls=%async_computation.3 | async-start | bytes 262144 | tf_op jit(solution)/shard_map/all_to_all | solution.py:108
  170.3 0.0 copy-done.1
  170.3 0.0 copy-done.2
  170.3 0.0 copy-done.3
  170.3 0.1 select_reduce_fusion
  170.4 5.2 %all-to-all-done.3 = bf16[8,2,4096]{2,1,0:T(2,128)(2,1)S(1)} async-done(((bf16[8,2,4096]{2,1,0:T(2,128)(2,1)}), bf16[8,2,4096]{2,1,0:T(2,128)(2,1)S(1)}, u32[]{:S(2)}, u32[]{:S(2)}) %all-to-all-start.3) | async-done | bytes 131104 | tf_op jit(solution)/shard_map/all_to_all | solution.py:108
  175.6 0.1 all_to_all.26
  175.6 0.8 fusion.22
  (2 shorter events, 0.0 us)
Async XLA Ops:
  0.0 84.0 %copy-start = (bf16[1,4096,128]{2,1,0:T(8,128)(2,1)S(1)}, bf16[1,4096,128]{2,1,0:T(8,128)(2,1)}, u32[]{:S(2)}) copy-start(bf16[1,4096,128]{2,1,0:T(8,128)(2,1)} %param.11) | copy-start | bytes 3145732
  3.8 15.4 %all-to-all-start = ((f16[8,2,4224]{2,1,0:T(2,128)(2,1)}), f16[8,2,4224]{2,1,0:T(2,128)(2,1)S(1)}, u32[]{:S(2)}, u32[]{:S(2)}) async-start(f16[8,2,4224]{2,1,0:T(2,128)(2,1)} %all_to_all.20), calls=%async_computation | async-start | bytes 270336 | tf_op jit(solution)/shard_map/all_to_all | solution.py:88
  83.6 2.8 %copy-start.4 = (bf16[1,4096,128]{2,1,0:T(8,128)(2,1)S(1)}, bf16[1,4096,128]{2,1,0:T(8,128)(2,1)}, u32[]{:S(2)}) copy-start(bf16[1,4096,128]{2,1,0:T(8,128)(2,1)} %param.12) | copy-start | bytes 3145732
  89.0 81.3 %copy-start.1 = (s32[8,2]{0,1:T(2,128)S(1)}, s32[8,2]{0,1:T(2,128)}, u32[]{:S(2)}) copy-start(s32[8,2]{0,1:T(2,128)} %param.9) | copy-start | bytes 196
  89.0 81.3 %copy-start.2 = (s32[8,2]{0,1:T(2,128)S(1)}, s32[8,2]{0,1:T(2,128)}, u32[]{:S(2)}) copy-start(s32[8,2]{0,1:T(2,128)} %param.8) | copy-start | bytes 196
  89.0 81.3 %copy-start.3 = (f32[8,2]{0,1:T(2,128)S(1)}, f32[8,2]{0,1:T(2,128)}, u32[]{:S(2)}) copy-start(f32[8,2]{0,1:T(2,128)} %param.10) | copy-start | bytes 196
  89.0 30.6 %all-to-all-start.1 = ((bf16[8,8,64,128]{3,2,1,0:T(8,128)(2,1)}), bf16[8,8,64,128]{3,2,1,0:T(8,128)(2,1)}, u32[]{:S(2)}, u32[]{:S(2)}) async-start(bf16[8,8,64,128]{3,2,1,0:T(8,128)(2,1)} %bitcast.25), calls=%async_computation.1 | async-start | bytes 2097152 | tf_op jit(solution)/shard_map/all_to_all | solution.py:99
  152.4 23.2 %all-to-all-start.3 = ((bf16[8,2,4096]{2,1,0:T(2,128)(2,1)}), bf16[8,2,4096]{2,1,0:T(2,128)(2,1)S(1)}, u32[]{:S(2)}, u32[]{:S(2)}) async-start(bf16[8,2,4096]{2,1,0:T(2,128)(2,1)} %convert_element_type.62), calls=%async_computation.3 | async-start | bytes 262144 | tf_op jit(solution)/shard_map/all_to_all | solution.py:108

commit v3 on v2

--- a/solution.py
+++ b/solution.py
@@ -7,28 +7,8 @@
 
 CAP = 2
 BLOCK = 256
-LANES = 128
-STEPS = (64, 32, 16, 8)
 GROUP = ("x", "core")
 PLANE = ("z", "y")
-
-
-def raise_rows(peak):
-    k = jnp.zeros_like(peak)
-    for p in STEPS:
-        low = peak < 2.0 ** (15 - p)
-        peak = jnp.where(low, peak * 2.0**p, peak)
-        k = jnp.where(low, k + p, k)
-    return k
-
-
-def power(k, sign):
-    out = jnp.ones_like(k)
-    for p in STEPS:
-        low = k >= p
-        out = jnp.where(low, out * 2.0 ** (sign * p), out)
-        k = jnp.where(low, k - p, k)
-    return out
 
 
 def down_kernel(h_ref, w_ref, o_ref, w_all):
@@ -64,7 +44,7 @@
 
 
 def shards(tokens, expert_ids, slots, mix_weights, w_gate, w_up, w_down):
-    tok_rows, width = tokens.shape
+    _, width = tokens.shape
     experts = lax.axis_size(GROUP)
     nz, ny = lax.axis_size("z"), lax.axis_size("y")
     slot_count = experts * CAP
@@ -78,20 +58,15 @@
         slots[None, :, :] == (slot_ids % CAP)[:, None, None]
     )
     table = jnp.any(matches, axis=2).astype(jnp.bfloat16)
-    wide = tokens.astype(jnp.float32)
-    k = raise_rows(jnp.max(jnp.abs(wide), axis=1, keepdims=True))
-    lifted = (wide * power(k, 1)).astype(jnp.bfloat16)
-    held = jnp.concatenate(
-        [lifted, jnp.broadcast_to(k, (tok_rows, LANES)).astype(jnp.bfloat16)], axis=1
-    )
-    outgoing = jnp.dot(table, held, preferred_element_type=jnp.float32).astype(jnp.float16)
+    outgoing = jnp.dot(table, tokens, preferred_element_type=jnp.float32)
+    root = jnp.sqrt(jnp.abs(outgoing * 2.0**29))
+    outgoing = jnp.where(outgoing < 0, -root, root).astype(jnp.float16)
     arrived = lax.all_to_all(outgoing, GROUP, split_axis=0, concat_axis=0, tiled=True)
     portion = lax.all_gather(arrived, PLANE, axis=0, tiled=True)
-    x = portion[:, :width].astype(jnp.bfloat16)
-    lower = power(portion[:, width : width + 1].astype(jnp.float32), -1)
-
-    gate = jnp.dot(x, w_gate[0], preferred_element_type=jnp.float32) * lower
-    up = jnp.dot(x, w_up[0], preferred_element_type=jnp.float32) * lower
+    root = portion.astype(jnp.float32)
+    x = (root * jnp.abs(root)).astype(jnp.bfloat16)
+    gate = jnp.dot(x, w_gate[0], preferred_element_type=jnp.float32) * 2.0**-29
+    up = jnp.dot(x, w_up[0], preferred_element_type=jnp.float32) * 2.0**-29
     hidden = jax.nn.silu(gate) * up
     packed = jnp.sqrt(jnp.sqrt(jnp.abs(hidden * 2.0**40)))
     packed = jnp.where(hidden < 0, -packed, packed).astype(jnp.float16)

time: 177 us -> 173 us (0.977)
  blocking collectives: 118 us -> 115 us
  other arithmetic: 4.36 us -> 2.05 us
    all_gather x1, blocking collectives: 64.3 us -> 61.9 us  [shards(): portion = lax.all_gather(arrived, PLANE, axis=0, tiled=True)]
where the time goes in v3:
time: 173 us
  blocking collectives  115 us (66%)
  starting transfers between devices  33.4 us (19%)
  waiting for transfers between devices  7.28 us (4%)
  matrix products  7 us (4%)
  local copies, waits for them, and re-layouts  4.84 us (3%)
  Pallas kernels  3.42 us (2%)
  other arithmetic  2.05 us (1%)
    all_gather x1, blocking collectives, shards(): portion = lax.all_gather(arrived, PLANE, axis=0, tiled=True)  61.9 us
    all_to_all x1, blocking collectives, shards(): part = lax.all_to_all(part, PLANE, split_axis=0, concat_axis=0, tiled=True)  28.6 us
    all_gather x1, blocking collectives, shards(): spread = lax.all_gather(packed, 'z', axis=0, tiled=False)  24.2 us
    all_to_all x1, starting transfers between devices, shards(): lax.all_to_all(result, GROUP, split_axis=0, concat_axis=0, tiled=True)  18.1 us
    all_to_all x1, starting transfers between devices, shards(): lax.all_to_all(outgoing, GROUP, split_axis=0, concat_axis=0, tiled=True)  10.1 us
    all_to_all x1, waiting for transfers between devices, shards(): lax.all_to_all(result, GROUP, split_axis=0, concat_axis=0, tiled=True)  5.17 us
    all_to_all x1, starting transfers between devices, shards(): wd = lax.all_to_all(wd, 'y', split_axis=0, concat_axis=0, tiled=True)  5.16 us
  transfers between devices with their start and end apart: 3, of which 2 were waited for; matrix products, arithmetic and copies ran while one was open for 2% of the time, Pallas kernels for 0%

profile of v3, /device:TPU:1, one launch (start us, length us, event | category | flops | bytes accessed | tf_op | source)
XLA Modules:
  0.0 172.8 jit_solution(7632986162717530468)
XLA Ops:
  0.0 0.0 copy-start
  0.0 0.9 fusion.25
  0.9 1.1 fusion.24
  2.0 0.7 all_to_all.20
  2.8 10.1 %all-to-all-start = ((f16[8,2,4096]{2,1,0:T(2,128)(2,1)}), f16[8,2,4096]{2,1,0:T(2,128)(2,1)S(1)}, u32[]{:S(2)}, u32[]{:S(2)}) async-start(f16[8,2,4096]{2,1,0:T(2,128)(2,1)} %all_to_all.20), calls=%async_computation | async-start | bytes 262144 | tf_op jit(solution)/shard_map/all_to_all | solution.py:64
  12.9 1.5 copy.22
  14.4 1.7 copy.24
  16.0 2.1 %all-to-all-done = f16[8,2,4096]{2,1,0:T(2,128)(2,1)S(1)} async-done(((f16[8,2,4096]{2,1,0:T(2,128)(2,1)}), f16[8,2,4096]{2,1,0:T(2,128)(2,1)S(1)}, u32[]{:S(2)}, u32[]{:S(2)}) %all-to-all-start) | async-done | bytes 131104 | tf_op jit(solution)/shard_map/all_to_all | solution.py:64
  18.1 0.1 all_to_all.22
  18.2 61.9 %all-gather.3 = f16[1024,4096]{1,0:T(8,128)(2,1)S(1)} all-gather(f16[16,4096]{1,0:T(8,128)(2,1)S(1)} %all_to_all.22), channel_id=1, replica_groups=mesh['x'=4,'core'=2,'z'=8,'y'=8] {'z','y'}, dimensions={0}, use_global_device_ids=true | all-gather | bytes 8519680 | tf_op jit(solution)/shard_map/all_gather | solution.py:65
  80.2 0.0 copy-done
  80.2 0.0 copy-start.4
  80.2 2.4 %fusion.8 = f32[1024,128]{1,0:T(8,128)S(1)} fusion(f16[1024,4096]{1,0:T(8,128)(2,1)S(1)} %all-gather.3, bf16[1,4096,128]{2,1,0:T(8,128)(2,1)S(1)} %copy-done), kind=kOutput, calls=%fused_computation.11 | convolution fusion | flops 1090650112 | bytes 9961472 | tf_op jit(solution)/shard_map/dot_general | solution.py:68
  82.5 0.0 copy-done.4
  82.5 2.7 %fusion.19 = f16[1024,128]{1,0:T(8,128)(2,1)S(1)} fusion(bf16[1,4096,128]{2,1,0:T(8,128)(2,1)S(1)} %copy-done.4, f16[1024,4096]{1,0:T(8,128)(2,1)S(1)} %all-gather.3, f32[1024,128]{1,0:T(8,128)S(1)} %fusion.8), kind=kOutput, calls=%fused_computation.19 | convolution fusion | flops 1092091904 | bytes 10223616 | tf_op jit(solution)/shard_map/dot_general | solution.py:69
  85.3 0.0 copy-start.1
  85.3 0.0 copy-start.2
  85.3 0.0 copy-start.3
  85.3 5.2 %all-to-all-start.1 = ((bf16[8,8,64,128]{3,2,1,0:T(8,128)(2,1)}), bf16[8,8,64,128]{3,2,1,0:T(8,128)(2,1)}, u32[]{:S(2)}, u32[]{:S(2)}) async-start(bf16[8,8,64,128]{3,2,1,0:T(8,128)(2,1)} %bitcast.26), calls=%async_computation.1 | async-start | bytes 2097152 | tf_op jit(solution)/shard_map/all_to_all | solution.py:74
  90.5 24.2 %all-gather.4 = f16[8192,128]{1,0:T(8,128)(2,1)S(1)} all-gather(f16[1024,128]{1,0:T(8,128)(2,1)S(1)} %fusion.19), channel_id=2, replica_groups=mesh['x'=4,'core'=2,'z'=8,'y'=8] {'z'}, dimensions={0}, use_global_device_ids=true | all-gather | bytes 2359296 | tf_op jit(solution)/shard_map/all_gather | solution.py:75
  114.6 0.9 fusion.6.h_ref
  115.6 0.0 all-to-all-done.1.w_ref
  115.6 3.4 %shard_map.73 = bf16[1024,512]{1,0:T(8,128)(2,1)S(1)} custom-call(bf16[8,1024,128]{2,1,0:T(8,128)(2,1)S(1)} %fusion.6.h_ref, bf16[8,8,64,128]{3,2,1,0:T(8,128)(2,1)} %all-to-all-done.1.w_ref), custom_call_target="tpu_custom_call" | custom-call | flops 1073741824 | bytes 4194304 | tf_op jit(solution)/shard_map/pallas_call | solution.py:33
  119.0 28.6 %all_to_all.31 = bf16[64,16,512]{2,1,0:T(8,128)(2,1)S(1)} all-to-all(bf16[64,16,512]{2,1,0:T(8,128)(2,1)S(1)} %bitcast.27), channel_id=1, replica_groups=mesh['x'=4,'core'=2,'z'=8,'y'=8] {'z','y'}, dimensions={0} | all-to-all | bytes 2097152 | tf_op jit(solution)/shard_map/all_to_all | solution.py:80
  147.7 0.2 bitcast_reduce_fusion
  147.8 0.1 copy.21
  147.9 0.7 convert_element_type.49
  148.6 18.1 %all-to-all-start.3 = ((bf16[8,2,4096]{2,1,0:T(2,128)(2,1)}), bf16[8,2,4096]{2,1,0:T(2,128)(2,1)S(1)}, u32[]{:S(2)}, u32[]{:S(2)}) async-start(bf16[8,2,4096]{2,1,0:T(2,128)(2,1)} %convert_element_type.49), calls=%async_computation.3 | async-start | bytes 262144 | tf_op jit(solution)/shard_map/all_to_all | solution.py:83
  166.7 0.0 copy-done.1
  166.7 0.0 copy-done.2
  166.7 0.0 copy-done.3
  166.7 0.1 select_reduce_fusion
  166.8 5.2 %all-to-all-done.3 = bf16[8,2,4096]{2,1,0:T(2,128)(2,1)S(1)} async-done(((bf16[8,2,4096]{2,1,0:T(2,128)(2,1)}), bf16[8,2,4096]{2,1,0:T(2,128)(2,1)S(1)}, u32[]{:S(2)}, u32[]{:S(2)}) %all-to-all-start.3) | async-done | bytes 131104 | tf_op jit(solution)/shard_map/all_to_all | solution.py:83
  172.0 0.1 all_to_all.26
  172.1 0.8 fusion.26
  (1 shorter events, 0.0 us)
Async XLA Ops:
  0.0 80.2 %copy-start = (bf16[1,4096,128]{2,1,0:T(8,128)(2,1)S(1)}, bf16[1,4096,128]{2,1,0:T(8,128)(2,1)}, u32[]{:S(2)}) copy-start(bf16[1,4096,128]{2,1,0:T(8,128)(2,1)} %param.11) | copy-start | bytes 3145732
  2.8 15.4 %all-to-all-start = ((f16[8,2,4096]{2,1,0:T(2,128)(2,1)}), f16[8,2,4096]{2,1,0:T(2,128)(2,1)S(1)}, u32[]{:S(2)}, u32[]{:S(2)}) async-start(f16[8,2,4096]{2,1,0:T(2,128)(2,1)} %all_to_all.20), calls=%async_computation | async-start | bytes 262144 | tf_op jit(solution)/shard_map/all_to_all | solution.py:64
  80.2 2.4 %copy-start.4 = (bf16[1,4096,128]{2,1,0:T(8,128)(2,1)S(1)}, bf16[1,4096,128]{2,1,0:T(8,128)(2,1)}, u32[]{:S(2)}) copy-start(bf16[1,4096,128]{2,1,0:T(8,128)(2,1)} %param.12) | copy-start | bytes 3145732
  85.3 81.5 %copy-start.1 = (s32[8,2]{0,1:T(2,128)S(1)}, s32[8,2]{0,1:T(2,128)}, u32[]{:S(2)}) copy-start(s32[8,2]{0,1:T(2,128)} %param.9) | copy-start | bytes 196
  85.3 81.5 %copy-start.2 = (s32[8,2]{0,1:T(2,128)S(1)}, s32[8,2]{0,1:T(2,128)}, u32[]{:S(2)}) copy-start(s32[8,2]{0,1:T(2,128)} %param.8) | copy-start | bytes 196
  85.3 81.5 %copy-start.3 = (f32[8,2]{0,1:T(2,128)S(1)}, f32[8,2]{0,1:T(2,128)}, u32[]{:S(2)}) copy-start(f32[8,2]{0,1:T(2,128)} %param.10) | copy-start | bytes 196
  85.3 30.3 %all-to-all-start.1 = ((bf16[8,8,64,128]{3,2,1,0:T(8,128)(2,1)}), bf16[8,8,64,128]{3,2,1,0:T(8,128)(2,1)}, u32[]{:S(2)}, u32[]{:S(2)}) async-start(bf16[8,8,64,128]{3,2,1,0:T(8,128)(2,1)} %bitcast.26), calls=%async_computation.1 | async-start | bytes 2097152 | tf_op jit(solution)/shard_map/all_to_all | solution.py:74
  148.6 23.4 %all-to-all-start.3 = ((bf16[8,2,4096]{2,1,0:T(2,128)(2,1)}), bf16[8,2,4096]{2,1,0:T(2,128)(2,1)S(1)}, u32[]{:S(2)}, u32[]{:S(2)}) async-start(bf16[8,2,4096]{2,1,0:T(2,128)(2,1)} %convert_element_type.49), calls=%async_computation.3 | async-start | bytes 262144 | tf_op jit(solution)/shard_map/all_to_all | solution.py:83

commit v4 on v3

--- a/solution.py
+++ b/solution.py
@@ -6,25 +6,21 @@
 from jax.sharding import Mesh, PartitionSpec as P
 
 CAP = 2
-BLOCK = 256
 GROUP = ("x", "core")
 PLANE = ("z", "y")
 
 
 def down_kernel(h_ref, w_ref, o_ref, w_all):
-    nz, rows, unit = h_ref.shape
+    nz, _, unit = h_ref.shape
     ny, _, cols, _ = w_ref.shape
     for z in range(nz):
         for y in range(ny):
             w_all[pl.ds(y * cols, cols), pl.ds(z * unit, unit)] = w_ref[y, z]
 
-    @pl.loop(0, rows // BLOCK)
-    def _(i):
-        at = pl.ds(pl.multiple_of(i * BLOCK, BLOCK), BLOCK)
-        h = jnp.concatenate([h_ref[z, at, :] for z in range(nz)], axis=1)
-        o_ref[at, :] = lax.dot_general(
-            h, w_all[...], (((1,), (1,)), ((), ())), preferred_element_type=jnp.float32
-        ).astype(o_ref.dtype)
+    h = jnp.concatenate([h_ref[z] for z in range(nz)], axis=1)
+    o_ref[...] = lax.dot_general(
+        h, w_all[...], (((1,), (1,)), ((), ())), preferred_element_type=jnp.float32
+    ).astype(o_ref.dtype)
 
 
 def down(h, w):
@@ -35,7 +31,7 @@
         out_shape=jax.ShapeDtypeStruct((rows, ny * cols), jnp.bfloat16),
         in_specs=[pl.BlockSpec(memory_space=pltpu.VMEM)] * 2,
         out_specs=pl.BlockSpec(memory_space=pltpu.VMEM),
-        compiler_params=pltpu.CompilerParams(vmem_limit_bytes=16 << 20),
+        compiler_params=pltpu.CompilerParams(vmem_limit_bytes=20 << 20),
         scratch_shapes=[pltpu.VMEM((ny * cols, nz * unit), jnp.bfloat16)],
         cost_estimate=pl.CostEstimate(
             flops=2 * rows * nz * unit * ny * cols, bytes_accessed=4 << 20, transcendentals=0
@@ -53,6 +49,8 @@
 
     wd = w_down[0].T.reshape(cols, nz, ny, unit).transpose(2, 1, 0, 3)
 
+    pair = jnp.concatenate([w_gate[0], w_up[0]], axis=1)
+
     slot_ids = jnp.arange(slot_count, dtype=jnp.int32)
     matches = (expert_ids[None, :, :] == (slot_ids // CAP)[:, None, None]) & (
         slots[None, :, :] == (slot_ids % CAP)[:, None, None]
@@ -65,8 +63,8 @@
     portion = lax.all_gather(arrived, PLANE, axis=0, tiled=True)
     root = portion.astype(jnp.float32)
     x = (root * jnp.abs(root)).astype(jnp.bfloat16)
-    gate = jnp.dot(x, w_gate[0], preferred_element_type=jnp.float32) * 2.0**-29
-    up = jnp.dot(x, w_up[0], preferred_element_type=jnp.float32) * 2.0**-29
+    both = jnp.dot(x, pair, preferred_element_type=jnp.float32) * 2.0**-29
+    gate, up = both[:, :unit], both[:, unit:]
     hidden = jax.nn.silu(gate) * up
     packed = jnp.sqrt(jnp.sqrt(jnp.abs(hidden * 2.0**40)))
     packed = jnp.where(hidden < 0, -packed, packed).astype(jnp.float16)

time: 173 us -> 168 us (0.971)
  matrix products: 7 us -> 3.47 us
  Pallas kernels: 3.42 us -> 1.36 us
    dot_general x2 -> x1, matrix products: 5.07 us -> 2.38 us  [shards(): both = jnp.dot(x, pair, preferred_element_type=jnp.float32) * 2.0 ** (-29)]
    pallas_call x1, Pallas kernels: 3.42 us -> 1.36 us  [down(): pl.pallas_call(down_kernel, out_shape=jax.ShapeDtypeStruct((rows, ny * co...]
where the time goes in v4:
time: 168 us
  blocking collectives  114 us (68%)
  starting transfers between devices  33.9 us (20%)
  waiting for transfers between devices  7.29 us (4%)
  local copies, waits for them, and re-layouts  4.89 us (3%)
  matrix products  3.47 us (2%)
  other arithmetic  2.48 us (1%)
    all_gather x1, blocking collectives, shards(): portion = lax.all_gather(arrived, PLANE, axis=0, tiled=True)  62.1 us
    all_to_all x1, blocking collectives, shards(): part = lax.all_to_all(part, PLANE, split_axis=0, concat_axis=0, tiled=True)  28 us
    all_gather x1, blocking collectives, shards(): spread = lax.all_gather(packed, 'z', axis=0, tiled=False)  24.2 us
    all_to_all x1, starting transfers between devices, shards(): lax.all_to_all(result, GROUP, split_axis=0, concat_axis=0, tiled=True)  18.8 us
    all_to_all x1, starting transfers between devices, shards(): lax.all_to_all(outgoing, GROUP, split_axis=0, concat_axis=0, tiled=True)  10.1 us
    all_to_all x1, waiting for transfers between devices, shards(): lax.all_to_all(result, GROUP, split_axis=0, concat_axis=0, tiled=True)  5.17 us
    all_to_all x1, starting transfers between devices, shards(): wd = lax.all_to_all(wd, 'y', split_axis=0, concat_axis=0, tiled=True)  5.04 us
  transfers between devices with their start and end apart: 3, of which 2 were waited for; matrix products, arithmetic and copies ran while one was open for 2% of the time, Pallas kernels for 0%

profile of v4, /device:TPU:1, one launch (start us, length us, event | category | flops | bytes accessed | tf_op | source)
XLA Modules:
  0.0 167.8 jit_solution(2925889350847253162)
XLA Ops:
  0.0 0.0 copy-start
  0.0 0.8 fusion.16
  0.8 0.0 copy-done
  0.8 0.3 fusion.15
  1.2 0.8 all_to_all.20
  1.9 10.1 %all-to-all-start = ((f16[8,2,4096]{2,1,0:T(2,128)(2,1)}), f16[8,2,4096]{2,1,0:T(2,128)(2,1)S(1)}, u32[]{:S(2)}, u32[]{:S(2)}) async-start(f16[8,2,4096]{2,1,0:T(2,128)(2,1)} %all_to_all.20), calls=%async_computation | async-start | bytes 262144 | tf_op jit(solution)/shard_map/all_to_all | solution.py:62
  12.0 1.5 copy.22
  13.5 1.6 copy.24
  15.2 2.1 %all-to-all-done = f16[8,2,4096]{2,1,0:T(2,128)(2,1)S(1)} async-done(((f16[8,2,4096]{2,1,0:T(2,128)(2,1)}), f16[8,2,4096]{2,1,0:T(2,128)(2,1)S(1)}, u32[]{:S(2)}, u32[]{:S(2)}) %all-to-all-start) | async-done | bytes 131104 | tf_op jit(solution)/shard_map/all_to_all | solution.py:62
  17.3 0.1 all_to_all.22
  17.4 0.0 copy-start.4
  17.4 0.0 copy-start.5
  17.4 62.1 %all-gather.3 = f16[1024,4096]{1,0:T(8,128)(2,1)S(1)} all-gather(f16[16,4096]{1,0:T(8,128)(2,1)S(1)} %all_to_all.22), channel_id=1, replica_groups=mesh['x'=4,'core'=2,'z'=8,'y'=8] {'z','y'}, dimensions={0}, use_global_device_ids=true | all-gather | bytes 8519680 | tf_op jit(solution)/shard_map/all_gather | solution.py:63
  79.4 0.0 copy-done.4
  79.4 0.0 copy-done.5
  79.5 2.4 %fusion.9 = f32[1024,256]{1,0:T(8,128)S(1)} fusion(bf16[4096,128]{1,0:T(8,128)(2,1)S(1)} %bitcast.26, bf16[4096,128]{1,0:T(8,128)(2,1)S(1)} %bitcast.27, f16[1024,4096]{1,0:T(8,128)(2,1)S(1)} %all-gather.3), kind=kOutput, calls=%fused_computation.13 | convolution fusion | flops 2168717312 | bytes 11534336 | tf_op jit(solution)/shard_map/dot_general | solution.py:66
  81.8 0.5 fusion.14
  82.3 5.0 %all-to-all-start.1 = ((bf16[8,8,64,128]{3,2,1,0:T(8,128)(2,1)}), bf16[8,8,64,128]{3,2,1,0:T(8,128)(2,1)S(1)}, u32[]{:S(2)}, u32[]{:S(2)}) async-start(bf16[8,8,64,128]{3,2,1,0:T(8,128)(2,1)} %bitcast.20), calls=%async_computation.1 | async-start | bytes 2097152 | tf_op jit(solution)/shard_map/all_to_all | solution.py:72
  87.4 24.2 %all-gather.4 = f16[8192,128]{1,0:T(8,128)(2,1)S(1)} all-gather(f16[1024,128]{1,0:T(8,128)(2,1)S(1)} %fusion.14), channel_id=2, replica_groups=mesh['x'=4,'core'=2,'z'=8,'y'=8] {'z'}, dimensions={0}, use_global_device_ids=true | all-gather | bytes 2359296 | tf_op jit(solution)/shard_map/all_gather | solution.py:73
  111.6 0.9 fusion.4.h_ref
  112.5 0.0 copy-start.1
  112.5 0.0 copy-start.2
  112.6 0.0 copy-start.3
  112.6 0.0 all-to-all-done.1.w_ref
  112.6 1.4 shard_map.73
  113.9 28.0 %all_to_all.31 = bf16[64,16,512]{2,1,0:T(8,128)(2,1)S(1)} all-to-all(bf16[64,16,512]{2,1,0:T(8,128)(2,1)S(1)} %bitcast.21), channel_id=1, replica_groups=mesh['x'=4,'core'=2,'z'=8,'y'=8] {'z','y'}, dimensions={0} | all-to-all | bytes 2097152 | tf_op jit(solution)/shard_map/all_to_all | solution.py:78
  142.0 0.2 bitcast_reduce_fusion
  142.1 0.1 copy.21
  142.2 0.7 convert_element_type.49
  142.9 18.8 %all-to-all-start.3 = ((bf16[8,2,4096]{2,1,0:T(2,128)(2,1)}), bf16[8,2,4096]{2,1,0:T(2,128)(2,1)S(1)}, u32[]{:S(2)}, u32[]{:S(2)}) async-start(bf16[8,2,4096]{2,1,0:T(2,128)(2,1)} %convert_element_type.49), calls=%async_computation.3 | async-start | bytes 262144 | tf_op jit(solution)/shard_map/all_to_all | solution.py:81
  161.7 0.0 copy-done.1
  161.7 0.0 copy-done.2
  161.7 0.0 copy-done.3
  161.7 0.1 select_reduce_fusion
  161.8 5.2 %all-to-all-done.3 = bf16[8,2,4096]{2,1,0:T(2,128)(2,1)S(1)} async-done(((bf16[8,2,4096]{2,1,0:T(2,128)(2,1)}), bf16[8,2,4096]{2,1,0:T(2,128)(2,1)S(1)}, u32[]{:S(2)}, u32[]{:S(2)}) %all-to-all-start.3) | async-done | bytes 131104 | tf_op jit(solution)/shard_map/all_to_all | solution.py:81
  167.0 0.1 all_to_all.26
  167.0 0.8 fusion.18
  (1 shorter events, 0.0 us)
Async XLA Ops:
  0.0 0.8 copy-start
  1.9 15.4 %all-to-all-start = ((f16[8,2,4096]{2,1,0:T(2,128)(2,1)}), f16[8,2,4096]{2,1,0:T(2,128)(2,1)S(1)}, u32[]{:S(2)}, u32[]{:S(2)}) async-start(f16[8,2,4096]{2,1,0:T(2,128)(2,1)} %all_to_all.20), calls=%async_computation | async-start | bytes 262144 | tf_op jit(solution)/shard_map/all_to_all | solution.py:62
  17.4 62.1 %copy-start.4 = (bf16[1,4096,128]{2,1,0:T(8,128)(2,1)S(1)}, bf16[1,4096,128]{2,1,0:T(8,128)(2,1)}, u32[]{:S(2)}) copy-start(bf16[1,4096,128]{2,1,0:T(8,128)(2,1)} %param.12) | copy-start | bytes 3145732
  17.4 62.1 %copy-start.5 = (bf16[1,4096,128]{2,1,0:T(8,128)(2,1)S(1)}, bf16[1,4096,128]{2,1,0:T(8,128)(2,1)}, u32[]{:S(2)}) copy-start(bf16[1,4096,128]{2,1,0:T(8,128)(2,1)} %param.11) | copy-start | bytes 3145732
  82.3 30.2 %all-to-all-start.1 = ((bf16[8,8,64,128]{3,2,1,0:T(8,128)(2,1)}), bf16[8,8,64,128]{3,2,1,0:T(8,128)(2,1)S(1)}, u32[]{:S(2)}, u32[]{:S(2)}) async-start(bf16[8,8,64,128]{3,2,1,0:T(8,128)(2,1)} %bitcast.20), calls=%async_computation.1 | async-start | bytes 2097152 | tf_op jit(solution)/shard_map/all_to_all | solution.py:72
  112.5 49.2 %copy-start.1 = (s32[8,2]{0,1:T(2,128)S(1)}, s32[8,2]{0,1:T(2,128)}, u32[]{:S(2)}) copy-start(s32[8,2]{0,1:T(2,128)} %param.9) | copy-start | bytes 196
  112.5 49.2 %copy-start.2 = (s32[8,2]{0,1:T(2,128)S(1)}, s32[8,2]{0,1:T(2,128)}, u32[]{:S(2)}) copy-start(s32[8,2]{0,1:T(2,128)} %param.8) | copy-start | bytes 196
  112.6 49.2 %copy-start.3 = (f32[8,2]{0,1:T(2,128)S(1)}, f32[8,2]{0,1:T(2,128)}, u32[]{:S(2)}) copy-start(f32[8,2]{0,1:T(2,128)} %param.10) | copy-start | bytes 196
  142.9 24.0 %all-to-all-start.3 = ((bf16[8,2,4096]{2,1,0:T(2,128)(2,1)}), bf16[8,2,4096]{2,1,0:T(2,128)(2,1)S(1)}, u32[]{:S(2)}, u32[]{:S(2)}) async-start(bf16[8,2,4096]{2,1,0:T(2,128)(2,1)} %convert_element_type.49), calls=%async_computation.3 | async-start | bytes 262144 | tf_op jit(solution)/shard_map/all_to_all | solution.py:81

commit v5 on v4

--- a/solution.py
+++ b/solution.py
@@ -44,6 +44,7 @@
     experts = lax.axis_size(GROUP)
     nz, ny = lax.axis_size("z"), lax.axis_size("y")
     slot_count = experts * CAP
+    rows = nz * ny * slot_count
     unit = w_gate.shape[2]
     cols = w_down.shape[2]
 
@@ -70,17 +71,19 @@
     packed = jnp.where(hidden < 0, -packed, packed).astype(jnp.float16)
     packed, wd = lax.optimization_barrier((packed, wd))
     wd = lax.all_to_all(wd, "y", split_axis=0, concat_axis=0, tiled=True)
-    spread = lax.all_gather(packed, "z", axis=0, tiled=False)
+    spread = lax.all_gather(packed.reshape(slot_count, -1, unit), "z", axis=0, tiled=True)
+    spread = spread.reshape(nz, rows, unit)
     spread = spread.astype(jnp.float32)
     h = (spread * jnp.abs(spread) * (spread * spread * 2.0**-40)).astype(jnp.bfloat16)
+    weights = jnp.sum(jnp.where(matches, mix_weights[None, :, :], 0.0), axis=2).astype(jnp.bfloat16)
+    h, weights = lax.optimization_barrier((h, weights))
     part = down(h, wd)
     part = part.reshape(nz * ny, slot_count, ny * cols)
     part = lax.all_to_all(part, PLANE, split_axis=0, concat_axis=0, tiled=True)
     part = part.reshape(nz, ny, slot_count, ny * cols).astype(jnp.float32).sum(axis=1)
     result = part.transpose(1, 0, 2).reshape(slot_count, width).astype(jnp.bfloat16)
     back = lax.all_to_all(result, GROUP, split_axis=0, concat_axis=0, tiled=True)
-    weights = jnp.sum(jnp.where(matches, mix_weights[None, :, :], 0.0), axis=2)
-    mixed = jnp.dot(weights.T, back.astype(jnp.float32), preferred_element_type=jnp.float32)
+    mixed = jnp.dot(weights.T, back, preferred_element_type=jnp.float32)
     return mixed.astype(jnp.bfloat16)
 
 

time: 168 us -> 167 us (level)
  blocking collectives: 114 us -> 137 us
  starting transfers between devices: 33.9 us -> 15.1 us
  waiting for transfers between devices: 7.29 us -> 2.11 us
    all_to_all x0 -> x1, blocking collectives: none -> 23.1 us  [shards(): lax.all_to_all(result, GROUP, split_axis=0, concat_axis=0, tiled=True)]
    all_to_all x1 -> x0, starting transfers between devices: 18.8 us -> none  [shards(): lax.all_to_all(result, GROUP, split_axis=0, concat_axis=0, tiled=True)]
    all_to_all x1 -> x0, waiting for transfers between devices: 5.17 us -> none  [shards(): lax.all_to_all(result, GROUP, split_axis=0, concat_axis=0, tiled=True)]
  transfers between devices with their start and end apart: 3 -> 2, of which waited for: 2 -> 1; matrix products, arithmetic and copies ran while one was open for 2% -> 3% of each run, Pallas kernels for 0% -> 0%
where the time goes in v5:
time: 167 us; the launch traced here: 166 us
  blocking collectives  137 us (82%)
  starting transfers between devices  15.1 us (9%)
  local copies, waits for them, and re-layouts  4.24 us (3%)
  matrix products  3.44 us (2%)
  other arithmetic  2.48 us (1%)
  waiting for transfers between devices  2.11 us (1%)
    all_gather x1, blocking collectives, shards(): portion = lax.all_gather(arrived, PLANE, axis=0, tiled=True)  62.1 us
    all_to_all x1, blocking collectives, shards(): part = lax.all_to_all(part, PLANE, split_axis=0, concat_axis=0, tiled=True)  28 us
    all_gather x1, blocking collectives, shards(): lax.all_gather(packed.reshape(slot_count, -1, unit), 'z', axis=0, tiled=T...  24.2 us
    all_to_all x1, blocking collectives, shards(): lax.all_to_all(result, GROUP, split_axis=0, concat_axis=0, tiled=True)  23.1 us
    all_to_all x1, starting transfers between devices, shards(): lax.all_to_all(outgoing, GROUP, split_axis=0, concat_axis=0, tiled=True)  10.1 us
    all_to_all x1, starting transfers between devices, shards(): wd = lax.all_to_all(wd, 'y', split_axis=0, concat_axis=0, tiled=True)  5.03 us
  transfers between devices with their start and end apart: 2, of which 1 were waited for; matrix products, arithmetic and copies ran while one was open for 3% of the time, Pallas kernels for 0%

profile of v5, /device:TPU:1, one launch (start us, length us, event | category | flops | bytes accessed | tf_op | source)
XLA Modules:
  0.0 166.3 jit_solution(16562583748794292059)
XLA Ops:
  0.0 0.0 copy-start
  0.0 0.8 fusion.16
  0.8 0.0 copy-done
  0.8 0.3 fusion.15
  1.2 0.8 all_to_all.20
  1.9 10.1 %all-to-all-start = ((f16[8,2,4096]{2,1,0:T(2,128)(2,1)}), f16[8,2,4096]{2,1,0:T(2,128)(2,1)S(1)}, u32[]{:S(2)}, u32[]{:S(2)}) async-start(f16[8,2,4096]{2,1,0:T(2,128)(2,1)} %all_to_all.20), calls=%async_computation | async-start | bytes 262144 | tf_op jit(solution)/shard_map/all_to_all | solution.py:63
  12.0 1.5 copy.22
  13.5 1.7 copy.24
  15.2 2.1 %all-to-all-done = f16[8,2,4096]{2,1,0:T(2,128)(2,1)S(1)} async-done(((f16[8,2,4096]{2,1,0:T(2,128)(2,1)}), f16[8,2,4096]{2,1,0:T(2,128)(2,1)S(1)}, u32[]{:S(2)}, u32[]{:S(2)}) %all-to-all-start) | async-done | bytes 131104 | tf_op jit(solution)/shard_map/all_to_all | solution.py:63
  17.3 0.1 all_to_all.22
  17.4 0.0 copy-start.4
  17.4 0.0 copy-start.5
  17.4 62.1 %all-gather.2 = f16[1024,4096]{1,0:T(8,128)(2,1)S(1)} all-gather(f16[16,4096]{1,0:T(8,128)(2,1)S(1)} %all_to_all.22), channel_id=1, replica_groups=mesh['x'=4,'core'=2,'z'=8,'y'=8] {'z','y'}, dimensions={0}, use_global_device_ids=true | all-gather | bytes 8519680 | tf_op jit(solution)/shard_map/all_gather | solution.py:64
  79.4 0.0 copy-done.4
  79.4 0.0 copy-done.5
  79.5 0.0 copy-start.1
  79.5 0.0 copy-start.2
  79.5 0.0 copy-start.3
  79.5 2.3 %fusion.9 = f32[1024,256]{1,0:T(8,128)S(1)} fusion(bf16[4096,128]{1,0:T(8,128)(2,1)S(1)} %bitcast.30, bf16[4096,128]{1,0:T(8,128)(2,1)S(1)} %bitcast.31, f16[1024,4096]{1,0:T(8,128)(2,1)S(1)} %all-gather.2), kind=kOutput, calls=%fused_computation.13 | convolution fusion | flops 2168717312 | bytes 11534336 | tf_op jit(solution)/shard_map/dot_general | solution.py:67
  81.9 0.5 fusion.14
  82.3 5.0 %all-to-all-start.1 = ((bf16[8,8,64,128]{3,2,1,0:T(8,128)(2,1)}), bf16[8,8,64,128]{3,2,1,0:T(8,128)(2,1)S(1)}, u32[]{:S(2)}, u32[]{:S(2)}) async-start(bf16[8,8,64,128]{3,2,1,0:T(8,128)(2,1)} %bitcast.22), calls=%async_computation.1 | async-start | bytes 2097152 | tf_op jit(solution)/shard_map/all_to_all | solution.py:73
  87.4 0.0 copy-done.1
  87.4 0.0 copy-done.2
  87.4 0.0 copy-done.3
  87.4 0.1 select_reduce_fusion
  87.5 24.2 %all-gather.3 = f16[128,64,128]{2,1,0:T(8,128)(2,1)S(1)} all-gather(f16[16,64,128]{2,1,0:T(8,128)(2,1)S(1)} %bitcast.27), channel_id=1, replica_groups=mesh['x'=4,'core'=2,'z'=8,'y'=8] {'z'}, dimensions={0}, use_global_device_ids=true | all-gather | bytes 2359296 | tf_op jit(solution)/shard_map/all_gather | solution.py:74
  111.7 0.9 fusion.4.h_ref
  112.6 0.0 all-to-all-done.1.w_ref
  112.6 1.4 shard_map.73
  114.0 28.0 %all_to_all.31 = bf16[64,16,512]{2,1,0:T(8,128)(2,1)S(1)} all-to-all(bf16[64,16,512]{2,1,0:T(8,128)(2,1)S(1)} %bitcast.24), channel_id=1, replica_groups=mesh['x'=4,'core'=2,'z'=8,'y'=8] {'z','y'}, dimensions={0} | all-to-all | bytes 2097152 | tf_op jit(solution)/shard_map/all_to_all | solution.py:82
  142.0 0.2 bitcast_reduce_fusion
  142.2 0.1 copy.21
  142.3 0.1 convert_element_type.56
  142.4 23.1 %all_to_all.32 = bf16[8,2,4096]{2,1,0:T(2,128)(2,1)S(1)} all-to-all(bf16[8,2,4096]{2,1,0:T(2,128)(2,1)S(1)} %convert_element_type.56), channel_id=1, replica_groups=mesh['x'=4,'core'=2,'z'=8,'y'=8] {'x','core'}, dimensions={0} | all-to-all | bytes 262144 | tf_op jit(solution)/shard_map/all_to_all | solution.py:85
  165.5 0.1 all_to_all.26
  165.5 0.8 convolution_convert_fusion
  (1 shorter events, 0.0 us)
Async XLA Ops:
  0.0 0.8 copy-start
  1.9 15.4 %all-to-all-start = ((f16[8,2,4096]{2,1,0:T(2,128)(2,1)}), f16[8,2,4096]{2,1,0:T(2,128)(2,1)S(1)}, u32[]{:S(2)}, u32[]{:S(2)}) async-start(f16[8,2,4096]{2,1,0:T(2,128)(2,1)} %all_to_all.20), calls=%async_computation | async-start | bytes 262144 | tf_op jit(solution)/shard_map/all_to_all | solution.py:63
  17.4 62.1 %copy-start.4 = (bf16[1,4096,128]{2,1,0:T(8,128)(2,1)S(1)}, bf16[1,4096,128]{2,1,0:T(8,128)(2,1)}, u32[]{:S(2)}) copy-start(bf16[1,4096,128]{2,1,0:T(8,128)(2,1)} %param.12) | copy-start | bytes 3145732
  17.4 62.1 %copy-start.5 = (bf16[1,4096,128]{2,1,0:T(8,128)(2,1)S(1)}, bf16[1,4096,128]{2,1,0:T(8,128)(2,1)}, u32[]{:S(2)}) copy-start(bf16[1,4096,128]{2,1,0:T(8,128)(2,1)} %param.11) | copy-start | bytes 3145732
  79.5 7.9 %copy-start.1 = (s32[8,2]{0,1:T(2,128)S(1)}, s32[8,2]{0,1:T(2,128)}, u32[]{:S(2)}) copy-start(s32[8,2]{0,1:T(2,128)} %param.9) | copy-start | bytes 196
  79.5 7.9 %copy-start.2 = (s32[8,2]{0,1:T(2,128)S(1)}, s32[8,2]{0,1:T(2,128)}, u32[]{:S(2)}) copy-start(s32[8,2]{0,1:T(2,128)} %param.8) | copy-start | bytes 196
  79.5 7.9 %copy-start.3 = (f32[8,2]{0,1:T(2,128)S(1)}, f32[8,2]{0,1:T(2,128)}, u32[]{:S(2)}) copy-start(f32[8,2]{0,1:T(2,128)} %param.10) | copy-start | bytes 196
  82.3 30.3 %all-to-all-start.1 = ((bf16[8,8,64,128]{3,2,1,0:T(8,128)(2,1)}), bf16[8,8,64,128]{3,2,1,0:T(8,128)(2,1)S(1)}, u32[]{:S(2)}, u32[]{:S(2)}) async-start(bf16[8,8,64,128]{3,2,1,0:T(8,128)(2,1)} %bitcast.22), calls=%async_computation.1 | async-start | bytes 2097152 | tf_op jit(solution)/shard_map/all_to_all | solution.py:73

commit v6 on v5

--- a/solution.py
+++ b/solution.py
@@ -44,7 +44,6 @@
     experts = lax.axis_size(GROUP)
     nz, ny = lax.axis_size("z"), lax.axis_size("y")
     slot_count = experts * CAP
-    rows = nz * ny * slot_count
     unit = w_gate.shape[2]
     cols = w_down.shape[2]
 
@@ -64,15 +63,15 @@
     portion = lax.all_gather(arrived, PLANE, axis=0, tiled=True)
     root = portion.astype(jnp.float32)
     x = (root * jnp.abs(root)).astype(jnp.bfloat16)
-    both = jnp.dot(x, pair, preferred_element_type=jnp.float32) * 2.0**-29
+    both = jnp.dot(x, pair, preferred_element_type=jnp.float32)
+    both, wd = lax.optimization_barrier((both, wd))
+    wd = lax.all_to_all(wd, "y", split_axis=0, concat_axis=0, tiled=True)
+    both = both * 2.0**-29
     gate, up = both[:, :unit], both[:, unit:]
     hidden = jax.nn.silu(gate) * up
     packed = jnp.sqrt(jnp.sqrt(jnp.abs(hidden * 2.0**40)))
     packed = jnp.where(hidden < 0, -packed, packed).astype(jnp.float16)
-    packed, wd = lax.optimization_barrier((packed, wd))
-    wd = lax.all_to_all(wd, "y", split_axis=0, concat_axis=0, tiled=True)
-    spread = lax.all_gather(packed.reshape(slot_count, -1, unit), "z", axis=0, tiled=True)
-    spread = spread.reshape(nz, rows, unit)
+    spread = lax.all_gather(packed, "z", axis=0, tiled=False)
     spread = spread.astype(jnp.float32)
     h = (spread * jnp.abs(spread) * (spread * spread * 2.0**-40)).astype(jnp.bfloat16)
     weights = jnp.sum(jnp.where(matches, mix_weights[None, :, :], 0.0), axis=2).astype(jnp.bfloat16)

time: 167 us -> 167 us (level)
  no operation moved by 1% of the time
where the time goes in v6:
time: 167 us; the launch traced here: 166 us
  blocking collectives  137 us (82%)
  starting transfers between devices  15.1 us (9%)
  local copies, waits for them, and re-layouts  4.24 us (3%)
  matrix products  3.42 us (2%)
  other arithmetic  2.55 us (2%)
  waiting for transfers between devices  2.11 us (1%)
    all_gather x1, blocking collectives, shards(): portion = lax.all_gather(arrived, PLANE, axis=0, tiled=True)  62.1 us
    all_to_all x1, blocking collectives, shards(): part = lax.all_to_all(part, PLANE, split_axis=0, concat_axis=0, tiled=True)  28 us
    all_gather x1, blocking collectives, shards(): spread = lax.all_gather(packed, 'z', axis=0, tiled=False)  24.2 us
    all_to_all x1, blocking collectives, shards(): lax.all_to_all(result, GROUP, split_axis=0, concat_axis=0, tiled=True)  23.1 us
    all_to_all x1, starting transfers between devices, shards(): lax.all_to_all(outgoing, GROUP, split_axis=0, concat_axis=0, tiled=True)  10.1 us
    all_to_all x1, starting transfers between devices, shards(): wd = lax.all_to_all(wd, 'y', split_axis=0, concat_axis=0, tiled=True)  5.03 us
  transfers between devices with their start and end apart: 2, of which 1 were waited for; matrix products, arithmetic and copies ran while one was open for 3% of the time, Pallas kernels for 0%

profile of v6, /device:TPU:1, one launch (start us, length us, event | category | flops | bytes accessed | tf_op | source)
XLA Modules:
  0.0 166.4 jit_solution(9457976768745332962)
XLA Ops:
  0.0 0.0 copy-start
  0.0 0.8 fusion.11
  0.8 0.0 copy-done
  0.8 0.3 fusion.10
  1.2 0.8 all_to_all.20
  1.9 10.1 %all-to-all-start = ((f16[8,2,4096]{2,1,0:T(2,128)(2,1)}), f16[8,2,4096]{2,1,0:T(2,128)(2,1)S(1)}, u32[]{:S(2)}, u32[]{:S(2)}) async-start(f16[8,2,4096]{2,1,0:T(2,128)(2,1)} %all_to_all.20), calls=%async_computation | async-start | bytes 262144 | tf_op jit(solution)/shard_map/all_to_all | solution.py:62
  12.0 1.5 copy.22
  13.5 1.7 copy.24
  15.2 2.1 %all-to-all-done = f16[8,2,4096]{2,1,0:T(2,128)(2,1)S(1)} async-done(((f16[8,2,4096]{2,1,0:T(2,128)(2,1)}), f16[8,2,4096]{2,1,0:T(2,128)(2,1)S(1)}, u32[]{:S(2)}, u32[]{:S(2)}) %all-to-all-start) | async-done | bytes 131104 | tf_op jit(solution)/shard_map/all_to_all | solution.py:62
  17.3 0.1 all_to_all.22
  17.4 0.0 copy-start.4
  17.4 0.0 copy-start.5
  17.4 62.1 %all-gather.3 = f16[1024,4096]{1,0:T(8,128)(2,1)S(1)} all-gather(f16[16,4096]{1,0:T(8,128)(2,1)S(1)} %all_to_all.22), channel_id=1, replica_groups=mesh['x'=4,'core'=2,'z'=8,'y'=8] {'z','y'}, dimensions={0}, use_global_device_ids=true | all-gather | bytes 8519680 | tf_op jit(solution)/shard_map/all_gather | solution.py:63
  79.4 0.0 copy-done.4
  79.4 0.0 copy-done.5
  79.5 0.0 copy-start.1
  79.5 0.0 copy-start.2
  79.5 0.0 copy-start.3
  79.5 2.3 %fusion.1 = f32[1024,256]{1,0:T(8,128)S(1)} fusion(f16[1024,4096]{1,0:T(8,128)(2,1)S(1)} %all-gather.3, bf16[4096,128]{1,0:T(8,128)(2,1)S(1)} %bitcast.26, bf16[4096,128]{1,0:T(8,128)(2,1)S(1)} %bitcast.27), kind=kOutput, calls=%fused_computation.2 | convolution fusion | flops 2168455168 | bytes 11534336 | tf_op jit(solution)/shard_map/dot_general | solution.py:66
  81.8 5.0 %all-to-all-start.1 = ((bf16[8,8,64,128]{3,2,1,0:T(8,128)(2,1)}), bf16[8,8,64,128]{3,2,1,0:T(8,128)(2,1)S(1)}, u32[]{:S(2)}, u32[]{:S(2)}) async-start(bf16[8,8,64,128]{3,2,1,0:T(8,128)(2,1)} %bitcast.20), calls=%async_computation.1 | async-start | bytes 2097152 | tf_op jit(solution)/shard_map/all_to_all | solution.py:68
  86.9 0.0 copy-done.1
  86.9 0.0 copy-done.2
  86.9 0.0 copy-done.3
  86.9 0.1 select_reduce_fusion
  87.0 0.1 broadcast_multiply_fusion
  87.0 0.5 fusion.9
  87.5 24.2 %all-gather.4 = f16[8192,128]{1,0:T(8,128)(2,1)S(1)} all-gather(f16[1024,128]{1,0:T(8,128)(2,1)S(1)} %fusion.9), channel_id=2, replica_groups=mesh['x'=4,'core'=2,'z'=8,'y'=8] {'z'}, dimensions={0}, use_global_device_ids=true | all-gather | bytes 2359296 | tf_op jit(solution)/shard_map/all_gather | solution.py:74
  111.7 0.9 fusion.4.h_ref
  112.7 0.0 all-to-all-done.1.w_ref
  112.7 1.4 shard_map.73
  114.1 28.0 %all_to_all.31 = bf16[64,16,512]{2,1,0:T(8,128)(2,1)S(1)} all-to-all(bf16[64,16,512]{2,1,0:T(8,128)(2,1)S(1)} %bitcast.21), channel_id=1, replica_groups=mesh['x'=4,'core'=2,'z'=8,'y'=8] {'z','y'}, dimensions={0} | all-to-all | bytes 2097152 | tf_op jit(solution)/shard_map/all_to_all | solution.py:81
  142.1 0.2 bitcast_reduce_fusion
  142.3 0.1 copy.21
  142.4 0.1 convert_element_type.52
  142.4 23.1 %all_to_all.32 = bf16[8,2,4096]{2,1,0:T(2,128)(2,1)S(1)} all-to-all(bf16[8,2,4096]{2,1,0:T(2,128)(2,1)S(1)} %convert_element_type.52), channel_id=1, replica_groups=mesh['x'=4,'core'=2,'z'=8,'y'=8] {'x','core'}, dimensions={0} | all-to-all | bytes 262144 | tf_op jit(solution)/shard_map/all_to_all | solution.py:84
  165.6 0.1 all_to_all.26
  165.6 0.8 convolution_convert_fusion
  (1 shorter events, 0.0 us)
Async XLA Ops:
  0.0 0.8 copy-start
  1.9 15.4 %all-to-all-start = ((f16[8,2,4096]{2,1,0:T(2,128)(2,1)}), f16[8,2,4096]{2,1,0:T(2,128)(2,1)S(1)}, u32[]{:S(2)}, u32[]{:S(2)}) async-start(f16[8,2,4096]{2,1,0:T(2,128)(2,1)} %all_to_all.20), calls=%async_computation | async-start | bytes 262144 | tf_op jit(solution)/shard_map/all_to_all | solution.py:62
  17.4 62.1 %copy-start.4 = (bf16[1,4096,128]{2,1,0:T(8,128)(2,1)S(1)}, bf16[1,4096,128]{2,1,0:T(8,128)(2,1)}, u32[]{:S(2)}) copy-start(bf16[1,4096,128]{2,1,0:T(8,128)(2,1)} %param.12) | copy-start | bytes 3145732
  17.4 62.1 %copy-start.5 = (bf16[1,4096,128]{2,1,0:T(8,128)(2,1)S(1)}, bf16[1,4096,128]{2,1,0:T(8,128)(2,1)}, u32[]{:S(2)}) copy-start(bf16[1,4096,128]{2,1,0:T(8,128)(2,1)} %param.11) | copy-start | bytes 3145732
  79.5 7.4 %copy-start.1 = (s32[8,2]{0,1:T(2,128)S(1)}, s32[8,2]{0,1:T(2,128)}, u32[]{:S(2)}) copy-start(s32[8,2]{0,1:T(2,128)} %param.9) | copy-start | bytes 196
  79.5 7.4 %copy-start.2 = (s32[8,2]{0,1:T(2,128)S(1)}, s32[8,2]{0,1:T(2,128)}, u32[]{:S(2)}) copy-start(s32[8,2]{0,1:T(2,128)} %param.8) | copy-start | bytes 196
  79.5 7.4 %copy-start.3 = (f32[8,2]{0,1:T(2,128)S(1)}, f32[8,2]{0,1:T(2,128)}, u32[]{:S(2)}) copy-start(f32[8,2]{0,1:T(2,128)} %param.10) | copy-start | bytes 196
  81.8 30.8 %all-to-all-start.1 = ((bf16[8,8,64,128]{3,2,1,0:T(8,128)(2,1)}), bf16[8,8,64,128]{3,2,1,0:T(8,128)(2,1)S(1)}, u32[]{:S(2)}, u32[]{:S(2)}) async-start(bf16[8,8,64,128]{3,2,1,0:T(8,128)(2,1)} %bitcast.20), calls=%async_computation.1 | async-start | bytes 2097152 | tf_op jit(solution)/shard_map/all_to_all | solution.py:68

commit v7 on v5

--- a/solution.py
+++ b/solution.py
@@ -10,31 +10,23 @@
 PLANE = ("z", "y")
 
 
-def down_kernel(h_ref, w_ref, o_ref, w_all):
-    nz, _, unit = h_ref.shape
-    ny, _, cols, _ = w_ref.shape
-    for z in range(nz):
-        for y in range(ny):
-            w_all[pl.ds(y * cols, cols), pl.ds(z * unit, unit)] = w_ref[y, z]
-
-    h = jnp.concatenate([h_ref[z] for z in range(nz)], axis=1)
+def down_kernel(h_ref, w_ref, o_ref):
+    h = jnp.concatenate([h_ref[i] for i in range(h_ref.shape[0])], axis=1)
     o_ref[...] = lax.dot_general(
-        h, w_all[...], (((1,), (1,)), ((), ())), preferred_element_type=jnp.float32
+        h, w_ref[...], (((1,), (1,)), ((), ())), preferred_element_type=jnp.float32
     ).astype(o_ref.dtype)
 
 
 def down(h, w):
-    nz, rows, unit = h.shape
-    ny, _, cols, _ = w.shape
+    parts, rows, unit = h.shape
     return pl.pallas_call(
         down_kernel,
-        out_shape=jax.ShapeDtypeStruct((rows, ny * cols), jnp.bfloat16),
+        out_shape=jax.ShapeDtypeStruct((rows, w.shape[0]), jnp.bfloat16),
         in_specs=[pl.BlockSpec(memory_space=pltpu.VMEM)] * 2,
         out_specs=pl.BlockSpec(memory_space=pltpu.VMEM),
         compiler_params=pltpu.CompilerParams(vmem_limit_bytes=20 << 20),
-        scratch_shapes=[pltpu.VMEM((ny * cols, nz * unit), jnp.bfloat16)],
         cost_estimate=pl.CostEstimate(
-            flops=2 * rows * nz * unit * ny * cols, bytes_accessed=4 << 20, transcendentals=0
+            flops=2 * rows * parts * unit * w.shape[0], bytes_accessed=4 << 20, transcendentals=0
         ),
     )(h, w)
 
@@ -44,11 +36,11 @@
     experts = lax.axis_size(GROUP)
     nz, ny = lax.axis_size("z"), lax.axis_size("y")
     slot_count = experts * CAP
-    rows = nz * ny * slot_count
     unit = w_gate.shape[2]
     cols = w_down.shape[2]
 
-    wd = w_down[0].T.reshape(cols, nz, ny, unit).transpose(2, 1, 0, 3)
+    wd = w_down[0].T.reshape(cols, nz, ny, unit).transpose(2, 0, 1, 3)
+    wd = wd.reshape(ny, cols, nz * unit)
 
     pair = jnp.concatenate([w_gate[0], w_up[0]], axis=1)
 
@@ -71,13 +63,12 @@
     packed = jnp.where(hidden < 0, -packed, packed).astype(jnp.float16)
     packed, wd = lax.optimization_barrier((packed, wd))
     wd = lax.all_to_all(wd, "y", split_axis=0, concat_axis=0, tiled=True)
-    spread = lax.all_gather(packed.reshape(slot_count, -1, unit), "z", axis=0, tiled=True)
-    spread = spread.reshape(nz, rows, unit)
+    spread = lax.all_gather(packed, "z", axis=0, tiled=False)
     spread = spread.astype(jnp.float32)
     h = (spread * jnp.abs(spread) * (spread * spread * 2.0**-40)).astype(jnp.bfloat16)
     weights = jnp.sum(jnp.where(matches, mix_weights[None, :, :], 0.0), axis=2).astype(jnp.bfloat16)
     h, weights = lax.optimization_barrier((h, weights))
-    part = down(h, wd)
+    part = down(h, wd.reshape(ny * cols, nz * unit))
     part = part.reshape(nz * ny, slot_count, ny * cols)
     part = lax.all_to_all(part, PLANE, split_axis=0, concat_axis=0, tiled=True)
     part = part.reshape(nz, ny, slot_count, ny * cols).astype(jnp.float32).sum(axis=1)

time: 167 us -> 169 us (1.012)
  blocking collectives: 137 us -> 140 us
    all_to_all x1, blocking collectives: 23.1 us -> 25.5 us  [shards(): lax.all_to_all(result, GROUP, split_axis=0, concat_axis=0, tiled=True)]
  transfers between devices with their start and end apart: 2 -> 2, of which waited for: 1 -> 1; matrix products, arithmetic and copies ran while one was open for 3% -> 2% of each run, Pallas kernels for 0% -> 0%
where the time goes in v7:
time: 169 us
  blocking collectives  140 us (83%)
  starting transfers between devices  15.1 us (9%)
  local copies, waits for them, and re-layouts  4 us (2%)
  matrix products  3.44 us (2%)
  other arithmetic  2.48 us (1%)
  waiting for transfers between devices  2.34 us (1%)
    all_gather x1, blocking collectives, shards(): portion = lax.all_gather(arrived, PLANE, axis=0, tiled=True)  62.1 us
    all_to_all x1, blocking collectives, shards(): part = lax.all_to_all(part, PLANE, split_axis=0, concat_axis=0, tiled=True)  28 us
    all_to_all x1, blocking collectives, shards(): lax.all_to_all(result, GROUP, split_axis=0, concat_axis=0, tiled=True)  25.5 us
    all_gather x1, blocking collectives, shards(): spread = lax.all_gather(packed, 'z', axis=0, tiled=False)  24.2 us
    all_to_all x1, starting transfers between devices, shards(): lax.all_to_all(outgoing, GROUP, split_axis=0, concat_axis=0, tiled=True)  10.1 us
    all_to_all x1, starting transfers between devices, shards(): wd = lax.all_to_all(wd, 'y', split_axis=0, concat_axis=0, tiled=True)  5.03 us
  transfers between devices with their start and end apart: 2, of which 1 were waited for; matrix products, arithmetic and copies ran while one was open for 2% of the time, Pallas kernels for 0%

profile of v7, /device:TPU:1, one launch (start us, length us, event | category | flops | bytes accessed | tf_op | source)
XLA Modules:
  0.0 168.6 jit_solution(8740591847776477474)
XLA Ops:
  0.0 0.0 copy-start
  0.0 0.8 fusion.16
  0.8 0.0 copy-done
  0.8 0.3 fusion.15
  1.2 0.8 all_to_all.20
  1.9 10.1 %all-to-all-start = ((f16[8,2,4096]{2,1,0:T(2,128)(2,1)}), f16[8,2,4096]{2,1,0:T(2,128)(2,1)S(1)}, u32[]{:S(2)}, u32[]{:S(2)}) async-start(f16[8,2,4096]{2,1,0:T(2,128)(2,1)} %all_to_all.20), calls=%async_computation | async-start | bytes 262144 | tf_op jit(solution)/shard_map/all_to_all | solution.py:55
  12.0 1.5 copy.23
  13.5 0.1 copy.21
  13.7 1.3 reshape.48
  14.9 2.3 %all-to-all-done = f16[8,2,4096]{2,1,0:T(2,128)(2,1)S(1)} async-done(((f16[8,2,4096]{2,1,0:T(2,128)(2,1)}), f16[8,2,4096]{2,1,0:T(2,128)(2,1)S(1)}, u32[]{:S(2)}, u32[]{:S(2)}) %all-to-all-start) | async-done | bytes 131104 | tf_op jit(solution)/shard_map/all_to_all | solution.py:55
  17.3 0.1 all_to_all.22
  17.4 0.0 copy-start.4
  17.4 0.0 copy-start.5
  17.4 62.1 %all-gather.3 = f16[1024,4096]{1,0:T(8,128)(2,1)S(1)} all-gather(f16[16,4096]{1,0:T(8,128)(2,1)S(1)} %all_to_all.22), channel_id=1, replica_groups=mesh['x'=4,'core'=2,'z'=8,'y'=8] {'z','y'}, dimensions={0}, use_global_device_ids=true | all-gather | bytes 8519680 | tf_op jit(solution)/shard_map/all_gather | solution.py:56
  79.4 0.0 copy-done.4
  79.4 0.0 copy-done.5
  79.5 0.0 copy-start.1
  79.5 0.0 copy-start.2
  79.5 0.0 copy-start.3
  79.5 2.3 %fusion.9 = f32[1024,256]{1,0:T(8,128)S(1)} fusion(bf16[4096,128]{1,0:T(8,128)(2,1)S(1)} %bitcast.29, bf16[4096,128]{1,0:T(8,128)(2,1)S(1)} %bitcast.30, f16[1024,4096]{1,0:T(8,128)(2,1)S(1)} %all-gather.3), kind=kOutput, calls=%fused_computation.13 | convolution fusion | flops 2168717312 | bytes 11534336 | tf_op jit(solution)/shard_map/dot_general | solution.py:59
  81.9 0.5 fusion.14
  82.3 5.0 %all-to-all-start.1 = ((bf16[8,64,1024]{2,1,0:T(8,128)(2,1)}), bf16[8,64,1024]{2,1,0:T(8,128)(2,1)S(1)}, u32[]{:S(2)}, u32[]{:S(2)}) async-start(bf16[8,64,1024]{2,1,0:T(8,128)(2,1)} %reshape.48), calls=%async_computation.1 | async-start | bytes 2097152 | tf_op jit(solution)/shard_map/all_to_all | solution.py:65
  87.4 0.0 copy-done.1
  87.4 0.0 copy-done.2
  87.4 0.0 copy-done.3
  87.4 0.1 select_reduce_fusion
  87.5 24.2 %all-gather.4 = f16[8192,128]{1,0:T(8,128)(2,1)S(1)} all-gather(f16[1024,128]{1,0:T(8,128)(2,1)S(1)} %fusion.14), channel_id=2, replica_groups=mesh['x'=4,'core'=2,'z'=8,'y'=8] {'z'}, dimensions={0}, use_global_device_ids=true | all-gather | bytes 2359296 | tf_op jit(solution)/shard_map/all_gather | solution.py:66
  111.7 0.9 fusion.4.h_ref
  112.6 0.0 all-to-all-done.1
  112.6 1.3 shard_map.73
  113.9 28.0 %all_to_all.31 = bf16[64,16,512]{2,1,0:T(8,128)(2,1)S(1)} all-to-all(bf16[64,16,512]{2,1,0:T(8,128)(2,1)S(1)} %bitcast.24), channel_id=1, replica_groups=mesh['x'=4,'core'=2,'z'=8,'y'=8] {'z','y'}, dimensions={0} | all-to-all | bytes 2097152 | tf_op jit(solution)/shard_map/all_to_all | solution.py:73
  141.9 0.2 bitcast_reduce_fusion
  142.1 0.1 copy.22
  142.2 0.1 convert_element_type.52
  142.3 25.5 %all_to_all.32 = bf16[8,2,4096]{2,1,0:T(2,128)(2,1)S(1)} all-to-all(bf16[8,2,4096]{2,1,0:T(2,128)(2,1)S(1)} %convert_element_type.52), channel_id=1, replica_groups=mesh['x'=4,'core'=2,'z'=8,'y'=8] {'x','core'}, dimensions={0} | all-to-all | bytes 262144 | tf_op jit(solution)/shard_map/all_to_all | solution.py:76
  167.8 0.1 all_to_all.26
  167.9 0.8 convolution_convert_fusion
  (1 shorter events, 0.0 us)
Async XLA Ops:
  0.0 0.8 copy-start
  1.9 15.4 %all-to-all-start = ((f16[8,2,4096]{2,1,0:T(2,128)(2,1)}), f16[8,2,4096]{2,1,0:T(2,128)(2,1)S(1)}, u32[]{:S(2)}, u32[]{:S(2)}) async-start(f16[8,2,4096]{2,1,0:T(2,128)(2,1)} %all_to_all.20), calls=%async_computation | async-start | bytes 262144 | tf_op jit(solution)/shard_map/all_to_all | solution.py:55
  17.4 62.1 %copy-start.4 = (bf16[1,4096,128]{2,1,0:T(8,128)(2,1)S(1)}, bf16[1,4096,128]{2,1,0:T(8,128)(2,1)}, u32[]{:S(2)}) copy-start(bf16[1,4096,128]{2,1,0:T(8,128)(2,1)} %param.12) | copy-start | bytes 3145732
  17.4 62.1 %copy-start.5 = (bf16[1,4096,128]{2,1,0:T(8,128)(2,1)S(1)}, bf16[1,4096,128]{2,1,0:T(8,128)(2,1)}, u32[]{:S(2)}) copy-start(bf16[1,4096,128]{2,1,0:T(8,128)(2,1)} %param.11) | copy-start | bytes 3145732
  79.5 7.9 %copy-start.1 = (s32[8,2]{0,1:T(2,128)S(1)}, s32[8,2]{0,1:T(2,128)}, u32[]{:S(2)}) copy-start(s32[8,2]{0,1:T(2,128)} %param.9) | copy-start | bytes 196
  79.5 7.9 %copy-start.2 = (s32[8,2]{0,1:T(2,128)S(1)}, s32[8,2]{0,1:T(2,128)}, u32[]{:S(2)}) copy-start(s32[8,2]{0,1:T(2,128)} %param.8) | copy-start | bytes 196
  79.5 7.9 %copy-start.3 = (f32[8,2]{0,1:T(2,128)S(1)}, f32[8,2]{0,1:T(2,128)}, u32[]{:S(2)}) copy-start(f32[8,2]{0,1:T(2,128)} %param.10) | copy-start | bytes 196
  82.3 30.3 %all-to-all-start.1 = ((bf16[8,64,1024]{2,1,0:T(8,128)(2,1)}), bf16[8,64,1024]{2,1,0:T(8,128)(2,1)S(1)}, u32[]{:S(2)}, u32[]{:S(2)}) async-start(bf16[8,64,1024]{2,1,0:T(8,128)(2,1)} %reshape.48), calls=%async_computation.1 | async-start | bytes 2097152 | tf_op jit(solution)/shard_map/all_to_all | solution.py:65
